TPU v7x, 512 devices: a whole 4x8x8 slice. The times are simulated.
512 devices in a mesh: tok: 64 (over y, x, core), ch: 8 (over z).
Axes of the slice: x: 4, y: 8, z: 8, core: 2. Of those that a mesh axis runs over, the one named last changes fastest.
Arguments:
- fields: float32 [16384, 1024], P('tok', 'ch'), may hold values from -20 to 20
- gain_one: float32 [1024], P('ch'), may hold values from 0.1 to 1.9
- tok_in_weight: float32 [3072, 16384], P('ch', 'tok'), may hold values from -0.046875 to 0.046875
- tok_in_bias: float32 [3072], P('ch'), may hold values from -3 to 3
- tok_out_weight: float32 [16384, 3072], P('tok', 'ch'), may hold values from -0.109375 to 0.109375
- gain_two: float32 [1024], P('ch'), may hold values from 0.1 to 1.9
- ch_in_weight: float32 [1024, 6144], P('tok', 'ch'), may hold values from -0.1875 to 0.1875
- ch_in_bias: float32 [6144], P('ch'), may hold values from -3 to 3
- ch_out_weight: float32 [6144, 1024], P('ch', 'tok'), may hold values from -0.078125 to 0.078125
Outputs:
- block_out: float32 [16384, 1024], P('tok', 'ch')
All inputs are finite; a program needn't handle non-finite values.
Results may differ from a plain program's by a relative error of at most 0.000086.
Values sent between devices are 32-bit elements; how exact they have to be, the bound alone decides.
A program may use at most 64 MiB of HBM per device.

v0:
```python
import jax
import jax.numpy as jnp
from jax import lax
from jax.sharding import PartitionSpec as P

epsilon = 1e-05
highest = lax.Precision.HIGHEST


def matmul(left, right):
    return jnp.dot(left, right, precision=highest, preferred_element_type=jnp.float32)


def shards(
    fields,
    gain_one,
    tok_in_weight,
    tok_in_bias,
    tok_out_weight,
    gain_two,
    ch_in_weight,
    ch_in_bias,
    ch_out_weight,
):
    tok_rows, ch_width = fields.shape
    channels = ch_width * lax.axis_size("ch")
    row_total = lax.psum(jnp.sum(fields, axis=1, keepdims=True), "ch")
    centred = fields - row_total / channels
    row_spread = lax.psum(jnp.sum(centred * centred, axis=1, keepdims=True), "ch")
    normed_part = centred * lax.rsqrt(row_spread / channels + epsilon) * gain_one
    normed = lax.all_gather(normed_part, "ch", axis=1, tiled=True)
    columns = normed
    summed_cols = lax.psum_scatter(
        lax.dot_general(
            columns,
            tok_in_weight,
            (((0,), (1,)), ((), ())),
            precision=highest,
            preferred_element_type=jnp.float32,
        ),
        "tok",
        scatter_dimension=0,
        tiled=True,
    )
    activated = jax.nn.gelu(summed_cols + tok_in_bias[None, :], approximate=False)
    partial_value = lax.dot_general(
        tok_out_weight,
        lax.all_gather(activated, "tok", axis=0, tiled=True),
        (((1,), (1,)), ((), ())),
        precision=highest,
        preferred_element_type=jnp.float32,
    )
    mixed_sum = lax.psum_scatter(partial_value, "ch", scatter_dimension=1, tiled=True)
    kept_rows = fields + mixed_sum
    row_total_two = lax.psum(jnp.sum(kept_rows, axis=1, keepdims=True), "ch")
    centred_two = kept_rows - row_total_two / channels
    row_spread_two = lax.psum(jnp.sum(centred_two * centred_two, axis=1, keepdims=True), "ch")
    normed_part_two = centred_two * lax.rsqrt(row_spread_two / channels + epsilon) * gain_two
    normed_two = lax.all_gather(normed_part_two, "ch", axis=1, tiled=True)
    columns = normed_two
    hidden_sum = matmul(columns, lax.all_gather(ch_in_weight, "tok", axis=0, tiled=True))
    activated_two = jax.nn.gelu(hidden_sum + ch_in_bias[None, :], approximate=False)
    channel_terms = matmul(activated_two, lax.all_gather(ch_out_weight, "tok", axis=1, tiled=True))
    return kept_rows + lax.psum_scatter(channel_terms, "ch", scatter_dimension=1, tiled=True)


def solution(mesh):
    in_specs = (
        P("tok", "ch"),
        P("ch"),
        P("ch", "tok"),
        P("ch"),
        P("tok", "ch"),
        P("ch"),
        P("tok", "ch"),
        P("ch"),
        P("ch", "tok"),
    )
    out_specs = P("tok", "ch")
    return jax.shard_map(shards, mesh=mesh, in_specs=in_specs, out_specs=out_specs, check_vma=False)
```

profile of v0, /device:TPU:6, one launch (start us, length us, event | category | flops | bytes accessed | tf_op | source)
XLA Modules:
  0.0 690.1 jit_solution(6796700619415421560)
XLA Ops:
  6.5 0.0 copy-start
  6.5 0.0 all-gather.6.cloned.1.call-start
  6.5 1.1 reduce_sum.36
  7.6 23.2 %psum.28 = f32[256,1]{0,1:T(1,128)S(1)} all-reduce(f32[256,1]{0,1:T(1,128)S(1)} %bitcast.25), channel_id=1, replica_groups=mesh['tok'=64,'ch'=8] {'ch'}, use_global_device_ids=true, to_apply=%region_1.0 | all-reduce | flops 256 | bytes 2048 | tf_op jit(solution)/shard_map/psum | solution.py:27
  30.8 1.1 multiply_reduce_fusion.1
  31.9 14.2 %psum.29 = f32[256,1]{0,1:T(1,128)S(1)} all-reduce(f32[256,1]{0,1:T(1,128)S(1)} %bitcast.26), channel_id=1, replica_groups=mesh['tok'=64,'ch'=8] {'ch'}, use_global_device_ids=true, to_apply=%region_3.0 | all-reduce | flops 256 | bytes 2048 | tf_op jit(solution)/shard_map/psum | solution.py:29
  46.1 1.7 multiply_multiply_fusion.6
  47.8 0.0 all-gather.6.cloned.1.call-update
  47.8 0.0 all-reduce.3.cloned.1.call-start
  47.9 40.3 %all-gather.6.cloned.1.call-done = f32[256,1024]{1,0:T(8,128)} async-done(((f32[256,128]{1,0:T(8,128)}), f32[256,1024]{1,0:T(8,128)}) %all-gather.6.cloned.1.call-update) | async-done | bytes 1048592 | tf_op jit(solution)/shard_map/all_gather | solution.py:31
  88.1 0.0 copy-done
  88.1 5.8 fusion.129
  94.0 0.0 all-reduce.3.cloned.1.call-update
  94.0 0.0 all-gather.8.cloned.1.call-start
  94.0 1.3 dynamic-slice
  96.0 196.0 %all-reduce.3.cloned.1.call-done = f32[1024,384]{1,0:T(8,128)} async-done(((f32[1024,384]{1,0:T(8,128)}), f32[1024,384]{1,0:T(8,128)}) %all-reduce.3.cloned.1.call-update) | async-done | bytes 1572880
  292.0 0.0 copy-done.4
  292.0 1.4 fusion.90
  293.4 0.0 all-gather.8.cloned.1.call-update
  293.4 0.0 reduce-scatter.3.cloned.1.call-start
  293.5 83.5 %all-gather.8.cloned.1.call-done = f32[1024,384]{1,0:T(8,128)} async-done(((f32[16,384]{1,0:T(8,128)}), f32[1024,384]{1,0:T(8,128)}) %all-gather.8.cloned.1.call-update) | async-done | bytes 1572880 | tf_op jit(solution)/shard_map/all_gather | solution.py:48
  377.0 0.0 copy-done.2
  377.0 4.2 convolution_bitcast_fusion
  381.2 0.0 reduce-scatter.3.cloned.1.call-update
  381.3 0.0 all-gather.12.cloned.1.call-start
  381.3 0.5 all-gather.12.cloned.1.call-update
  381.9 0.0 all-gather.10.cloned.1.call-start
  381.9 0.0 copy-done.1
  381.9 0.1 copy.16
  382.0 41.0 %reduce-scatter.3.cloned.1.call-done = f32[256,128]{0,1:T(8,128)} async-done(((f32[256,1024]{0,1:T(8,128)}), f32[256,128]{0,1:T(8,128)}) %reduce-scatter.3.cloned.1.call-update) | async-done | bytes 131088 | tf_op jit(solution)/shard_map/reduce_scatter | solution.py:53
  423.1 0.9 fusion.128
  424.0 15.4 %psum.30 = f32[256,1]{0,1:T(1,128)S(1)} all-reduce(f32[256,1]{0,1:T(1,128)S(1)} %bitcast.22), channel_id=1, replica_groups=mesh['tok'=64,'ch'=8] {'ch'}, use_global_device_ids=true, to_apply=%region_7.0 | all-reduce | flops 256 | bytes 2048 | tf_op jit(solution)/shard_map/psum | solution.py:55
  439.5 14.9 %psum.31 = f32[256,1]{0,1:T(1,128)S(1)} all-reduce(f32[256,1]{0,1:T(1,128)S(1)} %bitcast.27), channel_id=1, replica_groups=mesh['tok'=64,'ch'=8] {'ch'}, use_global_device_ids=true, to_apply=%region_9.0 | all-reduce | flops 256 | bytes 2048 | tf_op jit(solution)/shard_map/psum | solution.py:57
  454.4 0.0 copy-done.5
  454.4 0.7 multiply_multiply_fusion.5
  455.1 0.0 all-gather.10.cloned.1.call-update
  455.1 0.0 all-gather.14.cloned.1.call-start
  455.2 0.7 all-gather.14.cloned.1.call-update
  455.9 0.2 reduce-scatter.5.cloned.1.call-start
  456.1 50.1 %all-gather.12.cloned.1.call-done = f32[1024,768]{1,0:T(8,128)} async-done(((f32[16,768]{1,0:T(8,128)}), f32[1024,768]{1,0:T(8,128)}) %all-gather.12.cloned.1.call-update) | async-done | bytes 3145744 | tf_op jit(solution)/shard_map/all_gather | solution.py:61
  506.3 42.9 %all-gather.10.cloned.1.call-done = f32[256,1024]{0,1:T(8,128)} async-done(((f32[256,128]{0,1:T(8,128)}), f32[256,1024]{0,1:T(8,128)}) %all-gather.10.cloned.1.call-update) | async-done | bytes 1048592 | tf_op jit(solution)/shard_map/all_gather | solution.py:59
  549.2 5.0 convolution_add_fusion
  554.2 78.4 %all-gather.14.cloned.1.call-done = f32[768,1024]{0,1:T(8,128)} async-done(((f32[768,16]{0,1:T(8,128)}), f32[768,1024]{0,1:T(8,128)}) %all-gather.14.cloned.1.call-update) | async-done | bytes 3145744 | tf_op jit(solution)/shard_map/all_gather | solution.py:63
  632.6 7.3 %fusion.2 = f32[256,1024]{0,1:T(8,128)} fusion(f32[768,1024]{0,1:T(8,128)} %all-gather.14.cloned.1.call-done, f32[256,768]{1,0:T(8,128)S(1)} %convolution_add_fusion), kind=kOutput, calls=%fused_computation.5 | convolution fusion | flops 2428502016 | bytes 4980736 | tf_op jit(solution)/shard_map/dot_general | solution.py:11
  639.9 0.0 reduce-scatter.5.cloned.1.call-update
  639.9 41.6 %reduce-scatter.5.cloned.1.call-done = f32[256,128]{0,1:T(8,128)} async-done(((f32[256,1024]{0,1:T(8,128)}), f32[256,128]{0,1:T(8,128)}) %reduce-scatter.5.cloned.1.call-update) | async-done | bytes 131088 | tf_op jit(solution)/shard_map/reduce_scatter | solution.py:64
  681.6 0.9 add.49
  682.5 0.8 copy.18
  (11 shorter events, 0.1 us)
Async XLA Ops:
  6.5 81.6 %copy-start = (f32[384,256]{1,0:T(8,128)S(1)}, f32[384,256]{1,0:T(8,128)}, u32[]{:S(2)}) copy-start(f32[384,256]{1,0:T(8,128)} %param.11) | copy-start | bytes 1179652
  6.5 285.5 %copy-start.4 = (f32[384]{0:T(512)S(1)}, f32[384]{0:T(512)}, u32[]{:S(2)}) copy-start(f32[384]{0:T(512)} %param.12) | copy-start | bytes 4612
  6.5 370.5 %copy-start.2 = (f32[256,384]{1,0:T(8,128)S(1)}, f32[256,384]{1,0:T(8,128)}, u32[]{:S(2)}) copy-start(f32[256,384]{1,0:T(8,128)} %param.13) | copy-start | bytes 1179652
  6.5 81.6 %all-gather.6.cloned.1.call-start = ((), (), s32[]{:S(2)}) async-start(), calls=%async_computation.2 | async-start | bytes 1179648 | tf_op jit(solution)/shard_map/all_gather | solution.py:31
  47.8 244.2 %all-reduce.3.cloned.1.call-start = ((), (), s32[]{:S(2)}) async-start(), calls=%async_computation.9 | async-start | bytes 3145728
  94.0 288.0 %copy-start.1 = (f32[256,128]{1,0:T(8,128)S(1)}, f32[256,128]{1,0:T(8,128)}, u32[]{:S(2)}) copy-start(f32[256,128]{1,0:T(8,128)} %param.9) | copy-start | bytes 393220
  94.0 360.4 %copy-start.5 = (f32[128]{0:T(128)S(1)}, f32[128]{0:T(128)}, u32[]{:S(2)}) copy-start(f32[128]{0:T(128)} %param.14) | copy-start | bytes 1540
  94.0 455.2 %copy-start.3 = (f32[768]{0:T(1024)S(1)}, f32[768]{0:T(1024)}, u32[]{:S(2)}) copy-start(f32[768]{0:T(1024)} %param.16) | copy-start | bytes 9220
  94.0 283.1 %all-gather.8.cloned.1.call-start = ((), (), s32[]{:S(2)}) async-start(), calls=%async_computation.3 | async-start | bytes 1597440 | tf_op jit(solution)/shard_map/all_gather | solution.py:48
  293.4 129.6 %reduce-scatter.3.cloned.1.call-start = ((), (), s32[]{:S(2)}) async-start(), calls=%async_computation.4 | async-start | bytes 1179648 | tf_op jit(solution)/shard_map/reduce_scatter | solution.py:53
  381.3 125.0 %all-gather.12.cloned.1.call-start = ((), (), s32[]{:S(2)}) async-start(), calls=%async_computation.6 | async-start | bytes 3194880 | tf_op jit(solution)/shard_map/all_gather | solution.py:61
  381.9 167.3 %all-gather.10.cloned.1.call-start = ((), (), s32[]{:S(2)}) async-start(), calls=%async_computation.5 | async-start | bytes 1179648 | tf_op jit(solution)/shard_map/all_gather | solution.py:59
  455.1 177.5 %all-gather.14.cloned.1.call-start = ((), (), s32[]{:S(2)}) async-start(), calls=%async_computation.7 | async-start | bytes 3194880 | tf_op jit(solution)/shard_map/all_gather | solution.py:63
  455.9 225.7 %reduce-scatter.5.cloned.1.call-start = ((), (), s32[]{:S(2)}) async-start(), calls=%async_computation.8 | async-start | bytes 1179648 | tf_op jit(solution)/shard_map/reduce_scatter | solution.py:64
Sparse Core Ops, SparseCore 0:
  47.9 40.1 all-gather.5
  94.1 197.8 all-reduce.2
  295.4 81.6 all-gather.7
  381.4 41.6 reduce-scatter.2
  426.2 79.9 all-gather.11
  508.2 40.9 all-gather.9
  552.5 80.0 all-gather.13
  640.1 41.4 reduce-scatter.4
where the time goes:
time: 691 us; the launch traced here: 690 us
  waiting for transfers between devices  575 us (83%)
  blocking collectives  67.7 us (10%)
  matrix products  22.3 us (3%)
  between operations  14.2 us (2%)
  other arithmetic  7.95 us (1%)
    unnamed x9, waiting for transfers between devices  197 us
    all_gather x1, waiting for transfers between devices, shards(): lax.all_gather(activated, 'tok', axis=0, tiled=True)  83.5 us
    all_gather x1, waiting for transfers between devices, shards(): lax.all_gather(ch_out_weight, 'tok', axis=1, tiled=True)  78.4 us
    all_gather x1, waiting for transfers between devices, shards(): lax.all_gather(ch_in_weight, 'tok', axis=0, tiled=True)  50.1 us
    all_gather x1, waiting for transfers between devices, shards(): normed_two = lax.all_gather(normed_part_two, 'ch', axis=1, tiled=True)  42.9 us
    reduce_scatter x1, waiting for transfers between devices, shards(): lax.psum_scatter(channel_terms, 'ch', scatter_dimension=1, tiled=True)  41.6 us
    reduce_scatter x1, waiting for transfers between devices, shards(): lax.psum_scatter(partial_value, 'ch', scatter_dimension=1, tiled=True)  41 us
    all_gather x1, waiting for transfers between devices, shards(): normed = lax.all_gather(normed_part, 'ch', axis=1, tiled=True)  40.3 us
  transfers between devices with their start and end apart: 8, of which 8 were waited for; matrix products, arithmetic and copies ran while one was open for 1% of the time, Pallas kernels for 0%

commit v1 on v0

v1 whole, which is shorter than its diff:
```python
import functools

import jax
import jax.numpy as jnp
from jax import lax
from jax.experimental import pallas as pl
from jax.experimental.pallas import tpu as pltpu
from jax.sharding import PartitionSpec as P

NY, NX = 8, 4
CORES = 2
MESH = pl.DeviceIdType.MESH
F32, BF16 = jnp.float32, jnp.bfloat16
EPSILON = 1e-05
LANES = 128


def split(value):
    high = value.astype(BF16)
    return high, (value - high.astype(F32)).astype(BF16)


def gelu(value):
    return 0.5 * value * (1.0 + lax.erf(value * 0.7071067811865476))


def dot3(a_high, a_low, b_high, b_low, dims):
    def one(a, b):
        return lax.dot_general(a, b, (dims, ((), ())), preferred_element_type=F32)

    return one(a_high, b_high) + (one(a_high, b_low) + one(a_low, b_high))


NN = ((1,), (0,))
NT = ((1,), (1,))


class Sender:
    def __init__(self, send_sem, recv_sem):
        self.send_sem, self.recv_sem = send_sem, recv_sem
        self.copies = []

    def __call__(self, src, dst, device):
        k = len(self.copies)
        copy = pltpu.make_async_remote_copy(
            src_ref=src,
            dst_ref=dst,
            send_sem=self.send_sem.at[k],
            recv_sem=self.recv_sem.at[k],
            device_id=device,
            device_id_type=MESH,
        )
        copy.start()
        self.copies.append(copy)
        return copy

    def finish(self):
        for copy in self.copies:
            copy.wait_send()


def wrap(value, n):
    return lax.rem(value + 2 * n, n)


def gather_ring(n, me, device, view, send, arrived=lambda src, h: None):
    half = n // 2
    flight = {}

    def take(d, s, h):
        flight.pop((d, s, h)).wait_recv()
        arrived(wrap(me - d * s, n), h)

    for s in range(1, half + 1):
        for h in (0, 1):
            for d in (1, -1):
                if s == half and (d == 1) != (h == 0):
                    continue
                if s > 1:
                    take(d, s - 1, h)
                block = view(wrap(me - d * (s - 1), n), h)
                flight[(d, s, h)] = send(block, block, device(wrap(me + d, n)))
        yield
    for key in sorted(flight, key=lambda k: (k[1], k[2])):
        take(*key)
    yield


def reduce_ring(n, me, device, part, slot, send, ready=lambda dst, dist: None):
    half = n // 2
    flight = {}

    def add(dst, d, t, h):
        flight.pop((d, t, h)).wait_recv()
        part(dst, h)[...] += slot(d, t, h)[...]

    for t in range(1, half + 1):
        dist = half + 1 - t
        ready(wrap(me + dist, n), dist)
        if dist != half:
            ready(wrap(me - dist, n), -dist)
        for h in (0, 1):
            for d in (1, -1):
                first = 1 if (d == 1) == (h == 0) else 2
                if t < first:
                    continue
                dst = wrap(me + d * dist, n)
                if t > first:
                    add(dst, d, t - 1, h)
                flight[(d, t, h)] = send(part(dst, h), slot(d, t, h), device(wrap(me + d, n)))
        yield
    ready(me, 0)
    for key in sorted(flight, key=lambda k: (k[1], k[2])):
        add(me, *key)
    yield


def slots_of(n):
    half = n // 2
    places = {}
    for t in range(1, half + 1):
        for h in (0, 1):
            for d in (1, -1):
                if t >= (1 if (d == 1) == (h == 0) else 2):
                    places[(d, t, h)] = len(places)
    return places


def kernel(
    nz, ny, nx,
    fields, gain_one, gain_two, tok_in, tok_bias, tok_out, ch_in, ch_bias, ch_out,
    out,
    gathered, kept, high, low, tok_in_f, tok_in_h, tok_in_l, tok_out_f, tok_out_h, tok_out_l,
    sums, sums_pair, sums_slot, sums_x, hidden, hidden_h, hidden_l,
    mixed, mixed_slot, ch_in_f, ch_in_h, ch_in_l, ch_out_f, ch_out_h, ch_out_l, act_h, act_l,
    final, final_slot, local_sem, send_sem, recv_sem,
):
    tok, z = lax.axis_index("tok"), lax.axis_index("ch")
    core = lax.rem(tok, CORES)
    chip = lax.div(tok, CORES)
    x, y = lax.rem(chip, nx), lax.div(chip, nx)
    rows = fields.shape[0]
    half_rows = rows // 2
    channels = nz * LANES
    x_width = channels // nx
    per_x = x_width // LANES
    y_rows = sums.shape[3]
    core_rows = ny * y_rows
    hidden_width = ch_in.shape[1]
    depth = ch_in.shape[0]

    def at_z(i):
        return (tok, i)

    def at_y(i):
        return ((i * nx + x) * CORES + core, z)

    def at_x(i):
        return ((y * nx + i) * CORES + core, z)

    partner = ((y * nx + x) * CORES + (1 - core), z)

    local = [
        pltpu.make_async_copy(fields, gathered.at[z, pl.ds(0, rows)], local_sem.at[0]),
        pltpu.make_async_copy(gain_one, gathered.at[z, pl.ds(rows, 1)], local_sem.at[1]),
        pltpu.make_async_copy(gain_two, gathered.at[z, pl.ds(rows + 1, 1)], local_sem.at[2]),
        pltpu.make_async_copy(ch_in, ch_in_f.at[core, y, x], local_sem.at[3]),
        pltpu.make_async_copy(ch_out, ch_out_f.at[core, x, y], local_sem.at[4]),
        pltpu.make_async_copy(tok_in, tok_in_f, local_sem.at[5]),
        pltpu.make_async_copy(tok_out, tok_out_f, local_sem.at[6]),
    ]
    for copy in local:
        copy.start()

    peers = [partner]
    if nz > 1:
        peers += [at_z(wrap(z + 1, nz)), at_z(wrap(z - 1, nz))]
    if ny > 1:
        peers += [at_y(wrap(y + 1, ny)), at_y(wrap(y - 1, ny))]
    peers += [at_x(wrap(x + k, nx)) for k in range(1, nx)]
    barrier = pltpu.get_barrier_semaphore()
    for peer in peers:
        pl.semaphore_signal(barrier, inc=1, device_id=peer, device_id_type=MESH)
    for copy in local[:5]:
        copy.wait()
    pl.semaphore_wait(barrier, len(peers))

    send = Sender(send_sem, recv_sem)

    def field_view(src, h):
        if h == 0:
            return gathered.at[src, pl.ds(0, half_rows)]
        return gathered.at[src, pl.ds(half_rows, half_rows + 8)]

    half_depth = depth // 2
    ring_fields = gather_ring(nz, z, at_z, field_view, send)
    ring_out_y = gather_ring(
        ny, y, at_y, lambda src, h: ch_out_f.at[core, x, src, pl.ds(h * half_depth, half_depth)], send
    )

    def in_to_partner(src, h):
        block = ch_in_f.at[core, src, :, pl.ds(h * half_depth, half_depth)]
        pair_copies.append(send(block, block, partner))

    def out_to_partner(src, h):
        block = ch_out_f.at[core, src, :, pl.ds(h * half_depth, half_depth)]
        pair_copies.append(send(block, block, partner))

    pair_copies = []
    ring_in_y = gather_ring(
        ny, y, at_y, lambda src, h: ch_in_f.at[core, src, :, pl.ds(h * half_depth, half_depth)], send, in_to_partner
    )
    ring_out_x = gather_ring(
        nx, x, at_x, lambda src, h: ch_out_f.at[core, src, :, pl.ds(h * half_depth, half_depth)], send, out_to_partner
    )

    next(ring_fields)
    own = ch_in_f.at[core, y, x]
    in_x = [send(own, own, at_x(wrap(x + k, nx))) for k in range(1, nx)]
    next(ring_out_y, None)
    for copy in local[5:]:
        copy.wait()

    def split_rows(source, high_ref, low_ref, step=32):
        def body(i, _):
            at = pl.ds(pl.multiple_of(i * step, step), step)
            high_ref[at, :], low_ref[at, :] = split(source[at, :])
            return 0

        lax.fori_loop(0, source.shape[0] // step, body, 0)

    split_rows(tok_in_f, tok_in_h, tok_in_l)
    split_rows(tok_out_f, tok_out_h, tok_out_l)
    for _ in ring_fields:
        next(ring_out_y, None)
    for _ in ring_out_y:
        pass
    for copy in in_x:
        copy.wait_recv()
    for h in (0, 1):
        in_to_partner(y, h)
        out_to_partner(x, h)
    next(ring_in_y)
    next(ring_out_x)

    def normalize(source, gain_row):
        step = 32

        def body(i, _):
            at = pl.ds(pl.multiple_of(i * step, step), step)
            blocks = [source[j, at, :] for j in range(nz)]
            mean = jnp.sum(sum(blocks[1:], blocks[0]), axis=1, keepdims=True) * (1.0 / channels)
            centred = [block - mean for block in blocks]
            squares = [block * block for block in centred]
            spread = jnp.sum(sum(squares[1:], squares[0]), axis=1, keepdims=True) * (1.0 / channels)
            scale = lax.rsqrt(spread + EPSILON)
            for j in range(nz):
                gain = gathered[j, pl.ds(gain_row, 1), :]
                columns = pl.ds(j * LANES, LANES)
                high[at, columns], low[at, columns] = split(centred[j] * scale * gain)
            return 0

        lax.fori_loop(0, rows // step, body, 0)

    normalize(gathered, rows)

    def hidden_sums(which):
        at = pl.ds(pl.multiple_of(which * core_rows, core_rows), core_rows)

        def body(j, _):
            columns = pl.ds(pl.multiple_of(j * x_width, x_width), x_width)
            result = dot3(tok_in_h[at, :], tok_in_l[at, :], high[:, columns], low[:, columns], NN)
            for i in range(ny):
                sums[which, i, j] = result[i * y_rows : (i + 1) * y_rows]
            return 0

        lax.fori_loop(0, nx, body, 0)

    half_y = ny // 2
    offsets = [half_y] if half_y else []
    for dist in range(half_y - 1, 0, -1):
        offsets += [dist, -dist]
    offsets.append(0)
    hidden_sums(1 - core)
    pair_sums = {}
    for k in offsets:
        dst = wrap(y + k, ny)
        pair_sums[k] = send(sums.at[1 - core, dst], sums_pair.at[dst], partner)
    hidden_sums(core)

    def sums_ready(dst, dist):
        pair_sums[dist].wait_recv()
        sums[core, dst] += sums_pair[dst]

    half_x = nx // 2
    y_slots = slots_of(ny)
    for _ in reduce_ring(
        ny,
        y,
        at_y,
        lambda dst, h: sums.at[core, dst, pl.ds(h * half_x, half_x)],
        lambda d, t, h: sums_slot.at[y_slots[(d, t, h)]],
        send,
        sums_ready,
    ):
        pass
    copies = []
    for k in range(1, nx):
        dst = wrap(x + k, nx)
        copies.append(send(sums.at[core, y, dst], sums_x.at[k - 1], at_x(dst)))
    total = sums[core, y, x]
    for k, copy in enumerate(copies):
        copy.wait_recv()
        total = total + sums_x[k]
    first = core * core_rows + y * y_rows
    shape = (y_rows, tok_bias.shape[1])
    wanted = lax.broadcasted_iota(jnp.int32, shape, 1) == lax.broadcasted_iota(jnp.int32, shape, 0) + first
    bias = jnp.sum(jnp.where(wanted, jnp.broadcast_to(tok_bias[...], shape), 0.0), axis=1, keepdims=True)
    hidden[core, y, x] = gelu(total + bias)

    own = hidden.at[core, y, x]
    copies = [send(own, own, at_x(wrap(x + k, nx))) for k in range(1, nx)]
    for copy in copies:
        copy.wait_recv()
    pair_hidden = []

    def hidden_view(src, h):
        return hidden.at[core, src, pl.ds(h * half_x, half_x)]

    def hidden_to_partner(src, h):
        block = hidden_view(src, h)
        pair_hidden.append(send(block, block, partner))

    ring = gather_ring(ny, y, at_y, hidden_view, send, hidden_to_partner)
    next(ring)
    for h in (0, 1):
        hidden_to_partner(y, h)
    for _ in ring:
        pass
    for copy in pair_hidden:
        copy.wait_recv()
    for c in range(CORES):

        def split_hidden(j, _):
            value = hidden[c, :, j].reshape(core_rows, x_width)
            for k in range(per_x):
                pair = split(value[:, k * LANES : (k + 1) * LANES])
                hidden_h[j * per_x + k, pl.ds(c * core_rows, core_rows)] = pair[0]
                hidden_l[j * per_x + k, pl.ds(c * core_rows, core_rows)] = pair[1]
            return 0

        lax.fori_loop(0, nx, split_hidden, 0)

    def mixed_ready(dst, dist):
        mixed[dst] = dot3(tok_out_h[...], tok_out_l[...], hidden_h[dst], hidden_l[dst], NN)

    z_slots = slots_of(nz)

    def row_half(ref):
        return lambda i, h: ref.at[i, pl.ds(h * half_rows, half_rows)]

    ring = reduce_ring(
        nz, z, at_z, row_half(mixed), lambda d, t, h: mixed_slot.at[z_slots[(d, t, h)]], send, mixed_ready
    )
    for k, _ in enumerate(ring):
        if k % 2 == 0:
            next(ring_in_y, None)
        else:
            next(ring_out_x, None)
    kept[z] = gathered[z, pl.ds(0, rows), :] + mixed[z]
    ring = gather_ring(nz, z, at_z, row_half(kept), send)
    for k, _ in enumerate(ring):
        if k % 2 == 0:
            next(ring_in_y, None)
        else:
            next(ring_out_x, None)
    for late in (ring_in_y, ring_out_x):
        for _ in late:
            pass
    for copy in pair_copies:
        copy.wait_recv()

    def split_weights(i, _):
        for c in range(CORES):
            for j in range(nx):
                row = ((i * nx + j) * CORES + c) * depth
                at = pl.ds(pl.multiple_of(row, depth), depth)
                ch_in_h[at, :], ch_in_l[at, :] = split(ch_in_f[c, i, j])
                ch_out_h[at, :], ch_out_l[at, :] = split(ch_out_f[c, j, i])
        return 0

    lax.fori_loop(0, ny, split_weights, 0)
    normalize(kept, rows + 1)

    width = 256

    def hidden_block(j, _):
        columns = pl.ds(pl.multiple_of(j * width, width), width)
        result = dot3(high[...], low[...], ch_in_h[:, columns], ch_in_l[:, columns], NN)
        act_h[:, columns], act_l[:, columns] = split(gelu(result + ch_bias[:, columns]))
        return 0

    lax.fori_loop(0, hidden_width // width, hidden_block, 0)

    def final_ready(dst, dist):
        at = pl.ds(pl.multiple_of(dst * LANES, LANES), LANES)
        final[dst] = dot3(act_h[...], act_l[...], ch_out_h[at, :], ch_out_l[at, :], NT)

    for _ in reduce_ring(
        nz, z, at_z, row_half(final), lambda d, t, h: final_slot.at[z_slots[(d, t, h)]], send, final_ready
    ):
        pass
    out[...] = kept[z] + final[z]
    send.finish()


COPIES = 256


def block(nz, ny, nx, fields, gain_one, tok_in, tok_bias, tok_out, gain_two, ch_in, ch_bias, ch_out):
    rows, hidden_tok = fields.shape[0], tok_in.shape[0]
    depth, hidden_width = ch_in.shape
    channels = nz * LANES
    y_rows = hidden_tok // (CORES * ny)
    x_width = channels // nx
    z_slots, y_slots = max(1, len(slots_of(nz))), max(1, len(slots_of(ny)))

    def vmem(*shape, kind=F32):
        return pltpu.VMEM(shape, kind)

    scratch = [
        vmem(nz, rows + 8, LANES),
        vmem(nz, rows, LANES),
        vmem(rows, channels, kind=BF16),
        vmem(rows, channels, kind=BF16),
        vmem(hidden_tok, rows),
        vmem(hidden_tok, rows, kind=BF16),
        vmem(hidden_tok, rows, kind=BF16),
        vmem(rows, hidden_tok),
        vmem(rows, hidden_tok, kind=BF16),
        vmem(rows, hidden_tok, kind=BF16),
        vmem(CORES, ny, nx, y_rows, x_width),
        vmem(ny, nx, y_rows, x_width),
        vmem(y_slots, nx // 2, y_rows, x_width),
        vmem(nx - 1, y_rows, x_width),
        vmem(CORES, ny, nx, y_rows, x_width),
        vmem(nz, hidden_tok, LANES, kind=BF16),
        vmem(nz, hidden_tok, LANES, kind=BF16),
        vmem(nz, rows, LANES),
        vmem(z_slots, rows // 2, LANES),
        vmem(CORES, ny, nx, depth, hidden_width),
        vmem(channels, hidden_width, kind=BF16),
        vmem(channels, hidden_width, kind=BF16),
        vmem(CORES, nx, ny, depth, hidden_width),
        vmem(channels, hidden_width, kind=BF16),
        vmem(channels, hidden_width, kind=BF16),
        vmem(rows, hidden_width, kind=BF16),
        vmem(rows, hidden_width, kind=BF16),
        vmem(nz, rows, LANES),
        vmem(z_slots, rows // 2, LANES),
        pltpu.SemaphoreType.DMA((7,)),
        pltpu.SemaphoreType.DMA((COPIES,)),
        pltpu.SemaphoreType.DMA((COPIES,)),
    ]
    hbm, near = pl.BlockSpec(memory_space=pl.ANY), pl.BlockSpec(memory_space=pltpu.VMEM)
    return pl.pallas_call(
        functools.partial(kernel, nz, ny, nx),
        out_shape=jax.ShapeDtypeStruct((rows, LANES), F32),
        in_specs=[hbm, hbm, hbm, hbm, near, hbm, hbm, near, hbm],
        out_specs=near,
        scratch_shapes=scratch,
        compiler_params=pltpu.CompilerParams(
            collective_id=0, has_side_effects=True, vmem_limit_bytes=48 * 1024 * 1024
        ),
    )(
        fields,
        gain_one.reshape(1, LANES),
        gain_two.reshape(1, LANES),
        tok_in,
        tok_bias.reshape(1, hidden_tok),
        tok_out,
        ch_in,
        ch_bias.reshape(1, hidden_width),
        ch_out.T,
    )


def solution(mesh):
    in_specs = (
        P("tok", "ch"),
        P("ch"),
        P("ch", "tok"),
        P("ch"),
        P("tok", "ch"),
        P("ch"),
        P("tok", "ch"),
        P("ch"),
        P("ch", "tok"),
    )
    body = functools.partial(block, mesh.shape["ch"], NY, NX)
    return jax.shard_map(body, mesh=mesh, in_specs=in_specs, out_specs=P("tok", "ch"), check_vma=False)
```

time: 691 us -> 141 us (0.20)
  waiting for transfers between devices: 575 us -> 0 us
  Pallas kernels: 0 us -> 132 us
  blocking collectives: 67.7 us -> 0 us
  matrix products: 22.3 us -> 0 us
  between operations: 14.2 us -> 0.02 us
  other arithmetic: 7.95 us -> 0 us
    all_gather x5 -> x0, waiting for transfers between devices: 295 us -> none  [the longest x1 83.5 us: shards(): lax.all_gather(activated, 'tok', axis=0, tiled=True)]
    unnamed x9 -> x0, waiting for transfers between devices: 197 us -> none
    pallas_call x0 -> x1, Pallas kernels: none -> 132 us  [block(): pl.pallas_call(functools.partial(kernel, nz, ny, nx), out_shape=jax.Shape...]
    reduce_scatter x2 -> x0, waiting for transfers between devices: 82.7 us -> none  [the longest x1 41.6 us: shards(): lax.psum_scatter(channel_terms, 'ch', scatter_dimension=1, tiled=True)]
    psum x4 -> x0, blocking collectives: 67.7 us -> none  [the longest x1 23.2 us: shards(): row_total = lax.psum(jnp.sum(fields, axis=1, keepdims=True), 'ch')]
    dot_general x4 -> x0, matrix products: 22.3 us -> none  [the longest x2 12.3 us: matmul(): jnp.dot(left, right, precision=highest, preferred_element_type=jnp.float32)]
  transfers between devices with their start and end apart: 8 -> 0, of which waited for: 8 -> 0; matrix products, arithmetic and copies ran while one was open for 1% -> 0% of each run, Pallas kernels for 0% -> 0%
where the time goes in v1:
time: 141 us; the launch traced here: 139 us
  Pallas kernels  132 us (94%)
  local copies, waits for them, and re-layouts  6.52 us (5%)
    pallas_call x1, Pallas kernels, block(): pl.pallas_call(functools.partial(kernel, nz, ny, nx), out_shape=jax.Shape...  132 us
    unnamed x19, local copies, waits for them, and re-layouts  6.51 us

profile of v1, /device:TPU:6, one launch (start us, length us, event | category | flops | bytes accessed | tf_op | source)
XLA Modules:
  0.0 139.0 jit_solution(9266800621212706374)
XLA Ops:
  0.0 0.0 copy-start.8
  0.0 0.0 copy-start.7
  0.0 0.7 copy-done.8
  0.7 0.0 copy-done.7
  0.7 0.0 copy-start.5
  0.7 0.0 copy-start.6
  0.7 0.6 copy-done.5
  1.4 0.0 copy-done.6
  1.4 0.0 copy-start
  1.4 1.0 copy-done
  2.4 0.0 copy-start.1
  2.4 1.0 copy-done.1
  3.4 0.0 copy-start.2
  3.4 0.9 copy-done.2
  4.3 0.0 copy-start.3
  4.3 0.8 copy-done.3
  5.1 0.0 copy-start.4
  5.1 0.8 copy-done.4
  5.9 132.5 %shard_map.91 = f32[256,128]{1,0:T(8,128)S(1)} custom-call(f32[256,128]{1,0:T(8,128)S(1)} %copy-done.2, f32[1,128]{1,0:T(1,128)S(1)} %bitcast.4, f32[1,128]{1,0:T(1,128)S(1)} %bitcast.5, f32[384,256]{1,0:T(8,128)S(1)} %copy-done, f32[1,384]{1,0:T(1,128)S(1)} %reshape.14.tok_bias, f32[256,384]{1,0:T(8,128)S(1)} %copy-done.1, f32[16,768]{1,0:T(8,128)S(1)} %copy-done.3, ...), custom_call_target="tpu_custom_call" | custom-call | tf_op jit(solution)/shard_map/pallas_call | solution.py:466
  138.4 0.7 copy.11
  (2 shorter events, 0.0 us)
Async XLA Ops:
  0.0 0.7 copy-start.8
  0.0 0.7 copy-start.7
  0.7 0.7 copy-start.5
  0.7 0.7 copy-start.6
  1.4 1.0 copy-start
  2.4 1.0 copy-start.1
  3.4 0.9 copy-start.2
  4.3 0.8 copy-start.3
  5.1 0.8 copy-start.4

commit v2 on v1

v2 whole, which is shorter than its diff:
```python
import functools

import jax
import jax.numpy as jnp
from jax import lax
from jax.experimental import pallas as pl
from jax.experimental.pallas import tpu as pltpu
from jax.sharding import PartitionSpec as P

NY, NX = 8, 4
CORES = 2
CHUNKS = 2
PIECES = 4
MESH = pl.DeviceIdType.MESH
F32, BF16 = jnp.float32, jnp.bfloat16
EPSILON = 1e-05
LANES = 128
GAINS = 8


def split(value):
    high = value.astype(BF16)
    return high, (value - high.astype(F32)).astype(BF16)


def gelu(value):
    return 0.5 * value * (1.0 + lax.erf(value * 0.7071067811865476))


def dot3(a_high, a_low, b_high, b_low, dims):
    def one(a, b):
        return lax.dot_general(a, b, (dims, ((), ())), preferred_element_type=F32)

    return one(a_high, b_high) + (one(a_high, b_low) + one(a_low, b_high))


NN = ((1,), (0,))
NT = ((1,), (1,))
SENDS, RECEIVES = 22, 299


class Sender:
    def __init__(self, send_sem, recv_sem):
        self.send_sem, self.recv_sem = send_sem, recv_sem
        self.groups, self.receives = {}, 0

    def receive(self):
        self.receives += 1
        return self.recv_sem.at[self.receives - 1]

    def __call__(self, group, src, dst, device, recv=None):
        copy = pltpu.make_async_remote_copy(
            src_ref=src,
            dst_ref=dst,
            send_sem=self.send_sem.at[self.groups.setdefault(group, len(self.groups))],
            recv_sem=self.receive() if recv is None else recv,
            device_id=device,
            device_id_type=MESH,
        )
        copy.start()
        return copy

    def finish(self, sizes):
        for group, k in self.groups.items():
            wait_for(sizes[group], self.send_sem.at[k])


def wait_for(like, sem):
    pltpu.make_async_copy(like, like, sem).wait()


def wrap(value, n):
    return lax.rem(value + 2 * n, n)


def gather_ring(n, me, device, view, send, group, arrived=lambda src, h: None, pieces=2):
    half = n // 2
    flight = {}

    def take(d, s, h):
        flight.pop((d, s, h)).wait_recv()
        arrived(wrap(me - d * s, n), h)

    for s in range(1, half + 1):
        for h in range(pieces):
            for d in (1, -1):
                if s == half and (d == 1) != (h < pieces // 2):
                    continue
                if s > 1:
                    take(d, s - 1, h)
                block = view(wrap(me - d * (s - 1), n), h)
                flight[(d, s, h)] = send(group, block, block, device(wrap(me + d, n)))
        yield
    for key in sorted(flight, key=lambda k: (k[1], k[2])):
        take(*key)


def reduce_ring(n, me, device, part, slot, send, group, ready=lambda dst, dist: None, pieces=2):
    half = n // 2
    flight = {}

    def add(dst, d, t, h):
        flight.pop((d, t, h)).wait_recv()
        part(dst, h)[...] += slot(d, t, h)[...]

    for t in range(1, half + 1):
        dist = half + 1 - t
        ready(wrap(me + dist, n), dist)
        if dist != half:
            ready(wrap(me - dist, n), -dist)
        for h in range(pieces):
            for d in (1, -1):
                first = 1 if (d == 1) == (h < pieces // 2) else 2
                if t < first:
                    continue
                dst = wrap(me + d * dist, n)
                if t > first:
                    add(dst, d, t - 1, h)
                flight[(d, t, h)] = send(group, part(dst, h), slot(d, t, h), device(wrap(me + d, n)))
        yield
    ready(me, 0)
    for key in sorted(flight, key=lambda k: (k[1], k[2])):
        add(me, *key)


def reduce_two_stages(me, device, whole, half, slot, send, group, ready):
    n = 8
    flight = {}
    ready(wrap(me + 4, n), 4)
    for d in (1, -1):
        dst = wrap(me + 4 * d, n)
        flight[(d, 4)] = send(group, half(dst, d), slot(d, 4), device(wrap(me + 2 * d, n)))
    for d in (1, -1):
        dst = wrap(me + 3 * d, n)
        ready(dst, 3 * d)
        flight[(d, 3)] = send(group, whole(dst), slot(d, 3), device(wrap(me + d, n)))
    for d in (1, -1):
        dst = wrap(me + d, n)
        ready(dst, d)
        flight[(d, 1)] = send(group, whole(dst), slot(d, 1), device(dst))
    for d in (1, -1):
        ready(wrap(me + 2 * d, n), 2 * d)
    ready(me, 0)
    yield
    for d in (1, -1):
        dst = wrap(me + 2 * d, n)
        flight[(d, 3)].wait_recv()
        flight[(d, 4)].wait_recv()
        whole(dst)[...] += slot(d, 3)[...]
        half(dst, d)[...] += slot(d, 4)[...]
        flight[(d, 2)] = send(group, whole(dst), slot(d, 2), device(dst))
    yield
    for k in (1, 2):
        for d in (1, -1):
            flight[(d, k)].wait_recv()
            whole(me)[...] += slot(d, k)[...]


def gather_two_stages(me, device, whole, half, send, group, arrived):
    n = 8
    flight = {}
    own = whole(me)
    for k in (2, 1):
        for d in (1, -1):
            flight[(d, k)] = send(group, own, own, device(wrap(me + k * d, n)))
    yield
    for d in (1, -1):
        src = wrap(me - 2 * d, n)
        flight[(d, 2)].wait_recv()
        block = half(src, d)
        flight[(d, 4)] = send(group, block, block, device(wrap(me + 2 * d, n)))
        block = whole(src)
        flight[(d, 3)] = send(group, block, block, device(wrap(me + d, n)))
        arrived(block)
    for d in (1, -1):
        flight[(d, 1)].wait_recv()
        arrived(whole(wrap(me - d, n)))
    yield
    for d in (1, -1):
        flight[(d, 3)].wait_recv()
        arrived(whole(wrap(me - 3 * d, n)))
    for d in (1, -1):
        flight[(d, 4)].wait_recv()
        arrived(half(wrap(me - 4 * d, n), d))


def slots_of(n, pieces=2):
    half = n // 2
    places = {}
    for t in range(1, half + 1):
        for h in range(pieces):
            for d in (1, -1):
                if t >= (1 if (d == 1) == (h < pieces // 2) else 2):
                    places[(d, t, h)] = len(places)
    return places


def kernel(
    nz, ny, nx,
    fields, gain_one, gain_two, tok_in, tok_bias, tok_out, ch_in, ch_bias, ch_out,
    out,
    gathered, kept, high, low, tok_in_f, tok_in_h, tok_in_l, tok_out_f, tok_out_h, tok_out_l,
    sums_a, sums_b, pair_a, pair_b, slot_a, slot_ax, slot_bx, slot_by, hidden_a, hidden_b, hidden_h, hidden_l,
    mixed, mixed_slot, ch_in_f, ch_in_h, ch_in_l, ch_out_f, ch_out_h, ch_out_l, act_h, act_l,
    final, final_slot, tok_bias_v, ch_bias_v, local_sem, send_sem, recv_sem,
):
    tok, z = lax.axis_index("tok"), lax.axis_index("ch")
    core = lax.rem(tok, CORES)
    chip = lax.div(tok, CORES)
    x, y = lax.rem(chip, nx), lax.div(chip, nx)
    other = 1 - core
    rows = fields.shape[0]
    chunk_rows = rows // CHUNKS
    piece_rows = chunk_rows // PIECES
    channels = nz * LANES
    x_width = sums_a.shape[4]
    per_x = x_width // LANES
    y_rows = sums_a.shape[3]
    core_rows = ny * y_rows
    depth, hidden_width = ch_in.shape
    half_x, half_y = nx // 2, ny // 2

    def at_z(i):
        return (tok, i)

    def at_y(i):
        return ((i * nx + x) * CORES + core, z)

    def at_x(i):
        return ((y * nx + i) * CORES + core, z)

    partner = ((y * nx + x) * CORES + other, z)
    others_x = [wrap(x + k, nx) for k in range(1, nx)]
    others_y = [wrap(y + k, ny) for k in range(1, ny)]

    local = [
        pltpu.make_async_copy(source, target, local_sem.at[k])
        for k, (source, target) in enumerate(
            [
                (fields, gathered.at[z, pl.ds(GAINS, rows)]),
                (gain_one, gathered.at[z, pl.ds(0, 1)]),
                (gain_two, gathered.at[z, pl.ds(1, 1)]),
                (ch_in, ch_in_f.at[core, y, x]),
                (ch_out, ch_out_f.at[core, x, y]),
                (tok_in, tok_in_f),
                (tok_out, tok_out_f),
                (tok_bias, tok_bias_v.at[0]),
                (ch_bias, ch_bias_v.at[0]),
            ]
        )
    ]
    for copy in local:
        copy.start()

    peers = [partner] + [at_x(i) for i in others_x] + [at_y(i) for i in others_y]
    if nz > 1:
        peers += [at_z(wrap(z + 1, nz)), at_z(wrap(z - 1, nz))]
    barrier = pltpu.get_barrier_semaphore()
    for peer in peers:
        pl.semaphore_signal(barrier, inc=1, device_id=peer, device_id_type=MESH)
    for copy in local[:5]:
        copy.wait()
    pl.semaphore_wait(barrier, len(peers))

    send = Sender(send_sem, recv_sem)

    def field_view(c):
        def view(src, h):
            start = c * chunk_rows + h * piece_rows
            if start == 0:
                return gathered.at[src, pl.ds(0, piece_rows + GAINS)]
            return gathered.at[src, pl.ds(start + GAINS, piece_rows)]

        return view

    half_depth = depth // 2

    def depth_half(ref):
        return lambda src, h: ref.at[core, src, :, pl.ds(h * half_depth, half_depth)]

    pair_in_sem, pair_out_sem = send.receive(), send.receive()

    def in_to_partner(src, h):
        block = depth_half(ch_in_f)(src, h)
        send("pair in", block, block, partner, pair_in_sem)

    def out_to_partner(src, h):
        block = depth_half(ch_out_f)(src, h)
        send("pair out", block, block, partner, pair_out_sem)

    ring_fields = [gather_ring(nz, z, at_z, field_view(c), send, "fields", pieces=PIECES) for c in range(CHUNKS)]
    ring_out_y = gather_ring(
        ny, y, at_y, lambda src, h: ch_out_f.at[core, x, src, pl.ds(h * half_depth, half_depth)], send, "out y"
    )
    ring_in_y = gather_ring(ny, y, at_y, depth_half(ch_in_f), send, "in y", in_to_partner)
    ring_out_x = gather_ring(nx, x, at_x, depth_half(ch_out_f), send, "out x", out_to_partner)

    for ring in ring_fields:
        next(ring, None)
    own = ch_in_f.at[core, y, x]
    in_x_sem = send.receive()
    for i in others_x:
        send("in x", own, own, at_x(i), in_x_sem)
    next(ring_out_y, None)
    for copy in local[5:]:
        copy.wait()

    def split_rows(source, high_ref, low_ref, step=32):
        def body(i, _):
            at = pl.ds(pl.multiple_of(i * step, step), step)
            high_ref[at, :], low_ref[at, :] = split(source[at, :])
            return 0

        lax.fori_loop(0, source.shape[0] // step, body, 0)

    split_rows(tok_in_f, tok_in_h, tok_in_l)
    split_rows(tok_out_f, tok_out_h, tok_out_l)

    def normalize(c, source, offset, gain_row):
        step = 32

        def body(i, _):
            row = c * chunk_rows + i * step
            at = pl.ds(pl.multiple_of(row, step), step)
            blocks = [source[j, pl.ds(pl.multiple_of(row + offset, 8), step), :] for j in range(nz)]
            mean = jnp.sum(sum(blocks[1:], blocks[0]), axis=1, keepdims=True) * (1.0 / channels)
            centred = [block - mean for block in blocks]
            squares = [block * block for block in centred]
            spread = jnp.sum(sum(squares[1:], squares[0]), axis=1, keepdims=True) * (1.0 / channels)
            scale = lax.rsqrt(spread + EPSILON)
            for j in range(nz):
                gain = gathered[j, pl.ds(gain_row, 1), :]
                columns = pl.ds(j * LANES, LANES)
                high[at, columns], low[at, columns] = split(centred[j] * scale * gain)
            return 0

        lax.fori_loop(0, chunk_rows // step, body, 0)

    for s in range(2, nz // 2 + 1):
        for ring in ring_fields:
            next(ring)
        next(ring_out_y, None)
    for c, ring in enumerate(ring_fields):
        for _ in ring:
            pass
        if c == CHUNKS - 1:
            for _ in ring_out_y:
                pass
            if nx > 1:
                wait_for(ch_in_f.at[0, 0, pl.ds(0, nx - 1)], in_x_sem)
            for h in (0, 1):
                in_to_partner(y, h)
                out_to_partner(x, h)
            next(ring_in_y, None)
            next(ring_out_x, None)
        normalize(c, gathered, GAINS, 0)

    def hidden_sums(which, i):
        at = pl.ds(pl.multiple_of(which * core_rows, core_rows), core_rows)

        def body(j, _):
            start = i * (channels // 2) + 2 * j * x_width
            columns = pl.ds(pl.multiple_of(start, LANES), 2 * x_width)
            result = dot3(tok_in_h[at, :], tok_in_l[at, :], high[:, columns], low[:, columns], NN)
            for k in range(2):
                for r in range(ny):
                    piece = result[r * y_rows : (r + 1) * y_rows, k * x_width : (k + 1) * x_width]
                    if i == 0:
                        sums_a[which, r, 2 * j + k] = piece
                    else:
                        sums_b[which, 2 * j + k, r] = piece
            return 0

        lax.fori_loop(0, half_x, body, 0)

    offsets = [4, 3, -3, 1, -1, 2, -2, 0] if ny == 8 else [0]
    if ny != 8:
        for dist in range(1, half_y):
            offsets = [dist, -dist] + offsets
        offsets = ([half_y] if half_y else []) + offsets
    hidden_sums(other, 0)
    pair_sums = {}
    for k in offsets:
        dst = wrap(y + k, ny)
        pair_sums[k] = send("pair a", sums_a.at[other, dst], pair_a.at[dst], partner)
    hidden_sums(other, 1)
    pair_b_copies = []
    for i in others_x + [x]:
        pair_b_copies.append(send("pair b", sums_b.at[other, i], pair_b.at[i], partner))
    hidden_sums(core, 0)
    hidden_sums(core, 1)

    def sums_ready(dst, dist):
        pair_sums[dist].wait_recv()
        sums_a[core, dst] += pair_a[dst]

    y_slots = slots_of(ny)

    def sums_half(dst, h):
        return sums_a.at[core, dst, pl.ds(h * half_x, half_x)]

    if ny == 8:
        places = {1: 0, 2: 2, 3: 4}

        def y_slot(d, k):
            if k == 4:
                return slot_a.at[6, pl.ds((d < 0) * half_x, half_x)]
            return slot_a.at[places[k] + (d < 0)]

        ring = reduce_two_stages(
            y,
            at_y,
            lambda dst: sums_a.at[core, dst],
            lambda dst, d: sums_half(dst, int(d < 0)),
            y_slot,
            send,
            "sums y",
            sums_ready,
        )
    else:
        ring = reduce_ring(
            ny,
            y,
            at_y,
            sums_half,
            lambda d, t, h: slot_a.at[y_slots[(d, t, h)] // 2, pl.ds((y_slots[(d, t, h)] % 2) * half_x, half_x)],
            send,
            "sums y",
            sums_ready,
        )
    next(ring, None)
    bx_sem, by_sem, ax_sem = send.receive(), send.receive(), send.receive()
    for k, i in enumerate(others_x):
        pair_b_copies[k].wait_recv()
        sums_b[core, i] += pair_b[i]
        send("b x", sums_b.at[core, i], slot_bx.at[k], at_x(i), bx_sem)
    pair_b_copies[-1].wait_recv()
    sums_b[core, x] += pair_b[x]
    next(ring, None)
    if nx > 1:
        wait_for(slot_bx, bx_sem)

    def add_bx(r, _):
        total = sums_b[core, x, r]
        for k in range(nx - 1):
            total = total + slot_bx[k, r]
        sums_b[core, x, r] = total
        return 0

    lax.fori_loop(0, ny, add_bx, 0)
    for k, i in enumerate(others_y):
        send("b y", sums_b.at[core, x, i], slot_by.at[k], at_y(i), by_sem)
    for _ in ring:
        pass
    for k, i in enumerate(others_x):
        send("a x", sums_a.at[core, y, i], slot_ax.at[k], at_x(i), ax_sem)
    first = core * core_rows + y * y_rows
    shape = (y_rows, tok_bias_v.shape[1])
    wanted = lax.broadcasted_iota(jnp.int32, shape, 1) == lax.broadcasted_iota(jnp.int32, shape, 0) + first
    bias = jnp.sum(jnp.where(wanted, jnp.broadcast_to(tok_bias_v[...], shape), 0.0), axis=1, keepdims=True)
    if ny > 1:
        wait_for(slot_by, by_sem)
    total = sums_b[core, x, y]
    for k in range(ny - 1):
        total = total + slot_by[k]
    hidden_b[core, x, y] = gelu(total + bias)

    hb_y_sem, ha_x_sem, pair_ha_sem, pair_hb_sem = (send.receive() for _ in range(4))
    own = hidden_b.at[core, x, y]
    for i in others_y:
        send("hb y", own, own, at_y(i), hb_y_sem)
    if nx > 1:
        wait_for(slot_ax, ax_sem)
    total = sums_a[core, y, x]
    for k in range(nx - 1):
        total = total + slot_ax[k]
    hidden_a[core, y, x] = gelu(total + bias)
    own = hidden_a.at[core, y, x]
    for i in others_x:
        send("ha x", own, own, at_x(i), ha_x_sem)
    if nx > 1:
        wait_for(hidden_a.at[0, 0, pl.ds(0, nx - 1)], ha_x_sem)

    def hidden_view(src, h):
        return hidden_a.at[core, src, pl.ds(h * half_x, half_x)]

    def to_partner(block):
        send("pair ha", block, block, partner, pair_ha_sem)

    if ny == 8:
        ring = gather_two_stages(
            y,
            at_y,
            lambda src: hidden_a.at[core, src],
            lambda src, d: hidden_view(src, int(d < 0)),
            send,
            "ha y",
            to_partner,
        )
    else:
        ring = gather_ring(
            ny, y, at_y, hidden_view, send, "ha y", lambda src, h: to_partner(hidden_view(src, h))
        )
    next(ring, None)
    to_partner(hidden_a.at[core, y])
    if ny > 1:
        wait_for(hidden_b.at[0, 0, pl.ds(0, ny - 1)], hb_y_sem)
    own = hidden_b.at[core, x]
    hb_x = [send("hb x", own, own, at_x(i)) for i in others_x]
    send("pair hb", own, own, partner, pair_hb_sem)
    next(ring, None)
    for k, copy in enumerate(hb_x):
        copy.wait_recv()
        block = hidden_b.at[core, wrap(x - 1 - k, nx)]
        send("pair hb", block, block, partner, pair_hb_sem)
    for _ in ring:
        pass
    wait_for(hidden_b.at[0], pair_hb_sem)
    wait_for(hidden_a.at[0], pair_ha_sem)
    for c in range(CORES):

        def split_hidden(j, _, c=c):
            for i, value in enumerate((hidden_a[c, :, j], hidden_b[c, j])):
                value = value.reshape(core_rows, x_width)
                for k in range(per_x):
                    at = (i * (nz // 2) + j * per_x + k, pl.ds(c * core_rows, core_rows))
                    hidden_h[at], hidden_l[at] = split(value[:, k * LANES : (k + 1) * LANES])
            return 0

        lax.fori_loop(0, nx, split_hidden, 0)

    z_slots = slots_of(nz, PIECES)
    width = 256

    def split_out(i, _):
        for c in range(CORES):
            for j in range(nx):
                row = ((i * nx + j) * CORES + c) * depth
                at = pl.ds(pl.multiple_of(row, depth), depth)
                ch_out_h[at, :], ch_out_l[at, :] = split(ch_out_f[c, j, i])
        return 0

    def split_in(i, _):
        for c in range(CORES):
            for j in range(nx):
                row = ((i * nx + j) * CORES + c) * depth
                at = pl.ds(pl.multiple_of(row, depth), depth)
                ch_in_h[at, :], ch_in_l[at, :] = split(ch_in_f[c, i, j])
        return 0

    def stages(c):
        at = pl.ds(c * chunk_rows, chunk_rows)

        def mixed_ready(dst, dist):
            if c == 0:
                mixed[dst] = dot3(tok_out_h[...], tok_out_l[...], hidden_h[dst], hidden_l[dst], NN)

        def view(ref):
            return lambda i, h: ref.at[i, pl.ds(c * chunk_rows + h * piece_rows, piece_rows)]

        def slot(ref):
            return lambda d, t, h: ref.at[c, z_slots[(d, t, h)]]

        yield from reduce_ring(nz, z, at_z, view(mixed), slot(mixed_slot), send, "mixed", mixed_ready, PIECES)
        kept[z, at, :] = gathered[z, pl.ds(GAINS + c * chunk_rows, chunk_rows), :] + mixed[z, at, :]
        yield from gather_ring(nz, z, at_z, view(kept), send, "kept", pieces=PIECES)
        yield "weights"
        normalize(c, kept, 0, 1)

        def hidden_block(j, _):
            columns = pl.ds(pl.multiple_of(j * width, width), width)
            result = dot3(high[at, :], low[at, :], ch_in_h[:, columns], ch_in_l[:, columns], NN)
            act_h[at, columns], act_l[at, columns] = split(gelu(result + ch_bias_v[:, columns]))
            return 0

        lax.fori_loop(0, hidden_width // width, hidden_block, 0)

        def final_ready(dst, dist):
            wanted_rows = pl.ds(pl.multiple_of(dst * LANES, LANES), LANES)
            final[dst, at, :] = dot3(act_h[at, :], act_l[at, :], ch_out_h[wanted_rows, :], ch_out_l[wanted_rows, :], NT)

        yield from reduce_ring(nz, z, at_z, view(final), slot(final_slot), send, "final", final_ready, PIECES)
        out[at, :] = kept[z, at, :] + final[z, at, :]

    def weights():
        yield next(ring_in_y, None)
        yield next(ring_out_x, None)
        yield next(ring_in_y, None)
        for _ in ring_out_x:
            pass
        yield
        yield next(ring_in_y, None)
        wait_for(ch_out_f.at[0], pair_out_sem)
        lax.fori_loop(0, ny, split_out, 0)
        yield
        for _ in ring_in_y:
            pass
        yield
        wait_for(ch_in_f.at[0], pair_in_sem)
        lax.fori_loop(0, ny, split_in, 0)
        yield

    late = weights()
    chains = [stages(c) for c in range(CHUNKS)]
    step = 0
    while chains:
        for chain in list(chains):
            try:
                if next(chain) == "weights":
                    for _ in late:
                        pass
                    next(chain)
            except StopIteration:
                chains.remove(chain)
        next(late, None)
        step += 1
    send.finish(
        {
            "fields": gathered.at[pl.ds(0, nz - 1)],
            "mixed": mixed.at[pl.ds(0, nz - 1)],
            "kept": kept.at[pl.ds(0, nz - 1)],
            "final": final.at[pl.ds(0, nz - 1)],
            "out y": ch_out_f.at[0, 0, pl.ds(0, ny - 1)],
            "out x": ch_out_f.at[0, pl.ds(0, nx - 1)],
            "in x": ch_in_f.at[0, 0, pl.ds(0, nx - 1)],
            "in y": ch_in_f.at[0, pl.ds(0, ny - 1)],
            "pair in": ch_in_f.at[0],
            "pair out": ch_out_f.at[0],
            "pair a": pair_a,
            "pair b": pair_b,
            "sums y": sums_a.at[0, pl.ds(0, ny - 1)],
            "b x": slot_bx,
            "b y": slot_by,
            "a x": slot_ax,
            "hb y": hidden_b.at[0, 0, pl.ds(0, ny - 1)],
            "hb x": hidden_b.at[0, pl.ds(0, nx - 1)],
            "ha x": hidden_a.at[0, 0, pl.ds(0, nx - 1)],
            "ha y": hidden_a.at[0, pl.ds(0, ny - 1)],
            "pair ha": hidden_a.at[0],
            "pair hb": hidden_b.at[0],
        }
    )


def block(nz, ny, nx, fields, gain_one, tok_in, tok_bias, tok_out, gain_two, ch_in, ch_bias, ch_out):
    rows, hidden_tok = fields.shape[0], tok_in.shape[0]
    depth, hidden_width = ch_in.shape
    channels = nz * LANES
    y_rows = hidden_tok // (CORES * ny)
    x_width = channels // (2 * nx)
    z_slots = max(1, len(slots_of(nz, PIECES)))
    piece_rows = rows // (PIECES * CHUNKS)

    def vmem(*shape, kind=F32):
        return pltpu.VMEM(shape, kind)

    scratch = [
        vmem(nz, rows + GAINS, LANES),
        vmem(nz, rows, LANES),
        vmem(rows, channels, kind=BF16),
        vmem(rows, channels, kind=BF16),
        vmem(hidden_tok, rows),
        vmem(hidden_tok, rows, kind=BF16),
        vmem(hidden_tok, rows, kind=BF16),
        vmem(rows, hidden_tok),
        vmem(rows, hidden_tok, kind=BF16),
        vmem(rows, hidden_tok, kind=BF16),
        vmem(CORES, ny, nx, y_rows, x_width),
        vmem(CORES, nx, ny, y_rows, x_width),
        vmem(ny, nx, y_rows, x_width),
        vmem(nx, ny, y_rows, x_width),
        vmem(max(1, ny - 1), nx, y_rows, x_width),
        vmem(nx - 1, y_rows, x_width),
        vmem(nx - 1, ny, y_rows, x_width),
        vmem(max(1, ny - 1), y_rows, x_width),
        vmem(CORES, ny, nx, y_rows, x_width),
        vmem(CORES, nx, ny, y_rows, x_width),
        vmem(nz, hidden_tok, LANES, kind=BF16),
        vmem(nz, hidden_tok, LANES, kind=BF16),
        vmem(nz, rows, LANES),
        vmem(CHUNKS, z_slots, piece_rows, LANES),
        vmem(CORES, ny, nx, depth, hidden_width),
        vmem(channels, hidden_width, kind=BF16),
        vmem(channels, hidden_width, kind=BF16),
        vmem(CORES, nx, ny, depth, hidden_width),
        vmem(channels, hidden_width, kind=BF16),
        vmem(channels, hidden_width, kind=BF16),
        vmem(rows, hidden_width, kind=BF16),
        vmem(rows, hidden_width, kind=BF16),
        vmem(nz, rows, LANES),
        vmem(CHUNKS, z_slots, piece_rows, LANES),
        vmem(1, hidden_tok),
        vmem(1, hidden_width),
        pltpu.SemaphoreType.DMA((9,)),
        pltpu.SemaphoreType.DMA((SENDS,)),
        pltpu.SemaphoreType.DMA((RECEIVES,)),
    ]
    hbm = pl.BlockSpec(memory_space=pltpu.HBM)
    return pl.pallas_call(
        functools.partial(kernel, nz, ny, nx),
        out_shape=jax.ShapeDtypeStruct((rows, LANES), F32),
        in_specs=[hbm] * 9,
        out_specs=pl.BlockSpec(memory_space=pltpu.VMEM),
        scratch_shapes=scratch,
        compiler_params=pltpu.CompilerParams(
            collective_id=0, has_side_effects=True, vmem_limit_bytes=48 * 1024 * 1024
        ),
    )(
        *(
            pltpu.with_memory_space_constraint(argument, pltpu.HBM)
            for argument in (
                fields,
                gain_one.reshape(1, LANES),
                gain_two.reshape(1, LANES),
                tok_in,
                tok_bias,
                tok_out,
                ch_in,
                ch_bias,
                ch_out.T,
            )
        )
    )


def solution(mesh):
    in_specs = (
        P("tok", "ch"),
        P("ch"),
        P("ch", "tok"),
        P("ch"),
        P("tok", "ch"),
        P("ch"),
        P("tok", "ch"),
        P("ch"),
        P("ch", "tok"),
    )
    body = functools.partial(block, mesh.shape["ch"], NY, NX)
    return jax.shard_map(body, mesh=mesh, in_specs=in_specs, out_specs=P("tok", "ch"), check_vma=False)
```

time: 141 us -> 110 us (0.78); the launches traced: 139 us -> 110 us
  Pallas kernels: 132 us -> 109 us
  local copies, waits for them, and re-layouts: 6.52 us -> 0.66 us
    pallas_call x1, Pallas kernels: 132 us -> 109 us  [block(): pl.pallas_call(functools.partial(kernel, nz, ny, nx), out_shape=jax.Shape...]
    unnamed x19 -> x1, local copies, waits for them, and re-layouts: 6.51 us -> 0.66 us
where the time goes in v2:
time: 110 us
  Pallas kernels  109 us (99%)
    pallas_call x1, Pallas kernels, block(): pl.pallas_call(functools.partial(kernel, nz, ny, nx), out_shape=jax.Shape...  109 us

profile of v2, /device:TPU:6, one launch (start us, length us, event | category | flops | bytes accessed | tf_op | source)
XLA Modules:
  0.0 109.8 jit_solution(483899224297777700)
XLA Ops:
  0.0 109.1 %shard_map.91 = f32[256,128]{1,0:T(8,128)S(1)} custom-call(f32[256,128]{1,0:T(8,128)} %fields.1, f32[1,128]{1,0:T(1,128)} %bitcast.4, f32[1,128]{1,0:T(1,128)} %bitcast.5, f32[384,256]{1,0:T(8,128)} %tok_in.1, f32[384]{0:T(512)} %tok_bias.1, f32[256,384]{1,0:T(8,128)} %tok_out.1, f32[16,768]{1,0:T(8,128)} %ch_in.1, f32[768]{0:T(1024)} %ch_bias.1, ...), custom_call_target="tpu_custom_call" | custom-call | tf_op jit(solution)/shard_map/pallas_call | solution.py:699
  109.1 0.7 copy.11

commit v3 on v2

--- a/solution.py
+++ b/solution.py
@@ -36,17 +36,25 @@
 
 NN = ((1,), (0,))
 NT = ((1,), (1,))
-SENDS, RECEIVES = 22, 299
+SENDS, RECEIVES = 22, 188
 
 
 class Sender:
     def __init__(self, send_sem, recv_sem):
         self.send_sem, self.recv_sem = send_sem, recv_sem
-        self.groups, self.receives = {}, 0
+        self.groups, self.named, self.receives = {}, {}, 0
 
     def receive(self):
         self.receives += 1
         return self.recv_sem.at[self.receives - 1]
+
+    def shared(self, name):
+        def of(key):
+            if (name, key) not in self.named:
+                self.named[(name, key)] = self.receive()
+            return self.named[(name, key)]
+
+        return of
 
     def __call__(self, group, src, dst, device, recv=None):
         copy = pltpu.make_async_remote_copy(
@@ -73,7 +81,9 @@
     return lax.rem(value + 2 * n, n)
 
 
-def gather_ring(n, me, device, view, send, group, arrived=lambda src, h: None, pieces=2):
+def gather_ring(
+    n, me, device, view, send, group, arrived=lambda src, h: None, pieces=2, recv=lambda key: None, source=None
+):
     half = n // 2
     flight = {}
 
@@ -83,19 +93,24 @@
 
     for s in range(1, half + 1):
         for h in range(pieces):
+            first = source(h) if s == 1 and source else None
             for d in (1, -1):
                 if s == half and (d == 1) != (h < pieces // 2):
                     continue
                 if s > 1:
                     take(d, s - 1, h)
                 block = view(wrap(me - d * (s - 1), n), h)
-                flight[(d, s, h)] = send(group, block, block, device(wrap(me + d, n)))
+                flight[(d, s, h)] = send(
+                    group, block if first is None else first, block, device(wrap(me + d, n)), recv((d, s, h))
+                )
         yield
     for key in sorted(flight, key=lambda k: (k[1], k[2])):
         take(*key)
 
 
-def reduce_ring(n, me, device, part, slot, send, group, ready=lambda dst, dist: None, pieces=2):
+def reduce_ring(
+    n, me, device, part, slot, send, group, ready=lambda dst, dist: None, pieces=2, recv=lambda key: None
+):
     half = n // 2
     flight = {}
 
@@ -116,7 +131,9 @@
                 dst = wrap(me + d * dist, n)
                 if t > first:
                     add(dst, d, t - 1, h)
-                flight[(d, t, h)] = send(group, part(dst, h), slot(d, t, h), device(wrap(me + d, n)))
+                flight[(d, t, h)] = send(
+                    group, part(dst, h), slot(d, t, h), device(wrap(me + d, n)), recv((d, t, h))
+                )
         yield
     ready(me, 0)
     for key in sorted(flight, key=lambda k: (k[1], k[2])):
@@ -237,41 +254,61 @@
         pltpu.make_async_copy(source, target, local_sem.at[k])
         for k, (source, target) in enumerate(
             [
-                (fields, gathered.at[z, pl.ds(GAINS, rows)]),
-                (gain_one, gathered.at[z, pl.ds(0, 1)]),
-                (gain_two, gathered.at[z, pl.ds(1, 1)]),
+                (gain_one, gathered.at[z, pl.ds(chunk_rows, 1)]),
+                (gain_two, gathered.at[z, pl.ds(chunk_rows + 1, 1)]),
+                (
+                    fields.at[pl.ds(chunk_rows - piece_rows, piece_rows)],
+                    gathered.at[z, pl.ds(chunk_rows - piece_rows, piece_rows)],
+                ),
                 (ch_in, ch_in_f.at[core, y, x]),
                 (ch_out, ch_out_f.at[core, x, y]),
                 (tok_in, tok_in_f),
                 (tok_out, tok_out_f),
                 (tok_bias, tok_bias_v.at[0]),
                 (ch_bias, ch_bias_v.at[0]),
+                (
+                    fields.at[pl.ds(0, chunk_rows - piece_rows)],
+                    gathered.at[z, pl.ds(0, chunk_rows - piece_rows)],
+                ),
+                (
+                    fields.at[pl.ds(chunk_rows, rows - chunk_rows)],
+                    gathered.at[z, pl.ds(chunk_rows + GAINS, rows - chunk_rows)],
+                ),
             ]
         )
     ]
     for copy in local:
         copy.start()
 
-    peers = [partner] + [at_x(i) for i in others_x] + [at_y(i) for i in others_y]
+    peers = [partner] + [at_x(i) for i in others_x]
+    if ny > 1:
+        peers += [at_y(wrap(y + 1, ny)), at_y(wrap(y - 1, ny))]
     if nz > 1:
         peers += [at_z(wrap(z + 1, nz)), at_z(wrap(z - 1, nz))]
     barrier = pltpu.get_barrier_semaphore()
     for peer in peers:
         pl.semaphore_signal(barrier, inc=1, device_id=peer, device_id_type=MESH)
-    for copy in local[:5]:
-        copy.wait()
     pl.semaphore_wait(barrier, len(peers))
 
     send = Sender(send_sem, recv_sem)
 
     def field_view(c):
         def view(src, h):
-            start = c * chunk_rows + h * piece_rows
-            if start == 0:
-                return gathered.at[src, pl.ds(0, piece_rows + GAINS)]
-            return gathered.at[src, pl.ds(start + GAINS, piece_rows)]
+            start = c * (chunk_rows + GAINS) + h * piece_rows
+            extra = GAINS if (c, h) == (0, PIECES - 1) else 0
+            return gathered.at[src, pl.ds(start, piece_rows + extra)]
 
         return view
+
+    def field_source(c):
+        def source(h):
+            if (c, h) == (0, PIECES - 1):
+                for copy in local[:3]:
+                    copy.wait()
+                return field_view(c)(z, h)
+            return fields.at[pl.ds(c * chunk_rows + h * piece_rows, piece_rows)]
+
+        return source
 
     half_depth = depth // 2
 
@@ -288,7 +325,14 @@
         block = depth_half(ch_out_f)(src, h)
         send("pair out", block, block, partner, pair_out_sem)
 
-    ring_fields = [gather_ring(nz, z, at_z, field_view(c), send, "fields", pieces=PIECES) for c in range(CHUNKS)]
+    gather_sems = [send.shared(f"gather {c}") for c in range(CHUNKS)]
+    reduce_sems = [send.shared(f"reduce {c}") for c in range(CHUNKS)]
+    ring_fields = [
+        gather_ring(
+            nz, z, at_z, field_view(c), send, "fields", pieces=PIECES, recv=gather_sems[c], source=field_source(c)
+        )
+        for c in range(CHUNKS)
+    ]
     ring_out_y = gather_ring(
         ny, y, at_y, lambda src, h: ch_out_f.at[core, x, src, pl.ds(h * half_depth, half_depth)], send, "out y"
     )
@@ -297,6 +341,8 @@
 
     for ring in ring_fields:
         next(ring, None)
+    for copy in local[3:5]:
+        copy.wait()
     own = ch_in_f.at[core, y, x]
     in_x_sem = send.receive()
     for i in others_x:
@@ -317,24 +363,24 @@
     split_rows(tok_out_f, tok_out_h, tok_out_l)
 
     def normalize(c, source, offset, gain_row):
-        step = 32
-
-        def body(i, _):
-            row = c * chunk_rows + i * step
-            at = pl.ds(pl.multiple_of(row, step), step)
-            blocks = [source[j, pl.ds(pl.multiple_of(row + offset, 8), step), :] for j in range(nz)]
-            mean = jnp.sum(sum(blocks[1:], blocks[0]), axis=1, keepdims=True) * (1.0 / channels)
-            centred = [block - mean for block in blocks]
-            squares = [block * block for block in centred]
-            spread = jnp.sum(sum(squares[1:], squares[0]), axis=1, keepdims=True) * (1.0 / channels)
-            scale = lax.rsqrt(spread + EPSILON)
-            for j in range(nz):
-                gain = gathered[j, pl.ds(gain_row, 1), :]
-                columns = pl.ds(j * LANES, LANES)
-                high[at, columns], low[at, columns] = split(centred[j] * scale * gain)
-            return 0
-
-        lax.fori_loop(0, chunk_rows // step, body, 0)
+        at = pl.ds(c * chunk_rows, chunk_rows)
+
+        def block(j):
+            return source[j, pl.ds(c * chunk_rows + offset, chunk_rows), :]
+
+        total = block(0)
+        for j in range(1, nz):
+            total = total + block(j)
+        mean = jnp.sum(total, axis=1, keepdims=True) * (1.0 / channels)
+        total = jnp.square(block(0) - mean)
+        for j in range(1, nz):
+            total = total + jnp.square(block(j) - mean)
+        spread = jnp.sum(total, axis=1, keepdims=True) * (1.0 / channels)
+        scale = lax.rsqrt(spread + EPSILON)
+        for j in range(nz):
+            gain = gathered[j, pl.ds(gain_row, 1), :]
+            columns = pl.ds(j * LANES, LANES)
+            high[at, columns], low[at, columns] = split((block(j) - mean) * scale * gain)
 
     for s in range(2, nz // 2 + 1):
         for ring in ring_fields:
@@ -353,7 +399,7 @@
                 out_to_partner(x, h)
             next(ring_in_y, None)
             next(ring_out_x, None)
-        normalize(c, gathered, GAINS, 0)
+        normalize(c, gathered, c * GAINS, chunk_rows)
 
     def hidden_sums(which, i):
         at = pl.ds(pl.multiple_of(which * core_rows, core_rows), core_rows)
@@ -378,17 +424,28 @@
         for dist in range(1, half_y):
             offsets = [dist, -dist] + offsets
         offsets = ([half_y] if half_y else []) + offsets
+    far, near = ([4, 3, -3, 2], [-2, 1, -1, 0]) if ny == 8 else (list(range(1, ny)), [0])
+    hidden_sums(other, 1)
+    pair_b_copies = []
+    for i in others_x + [x]:
+        pair_b_copies.append(send("pair b", sums_b.at[other, i], pair_b.at[i], partner))
     hidden_sums(other, 0)
     pair_sums = {}
     for k in offsets:
         dst = wrap(y + k, ny)
         pair_sums[k] = send("pair a", sums_a.at[other, dst], pair_a.at[dst], partner)
-    hidden_sums(other, 1)
-    pair_b_copies = []
-    for i in others_x + [x]:
-        pair_b_copies.append(send("pair b", sums_b.at[other, i], pair_b.at[i], partner))
+    hidden_sums(core, 1)
+    bx_sems = [send.receive(), send.receive()]
+    by_sem, ax_sem = send.receive(), send.receive()
+    for k, i in enumerate(others_x):
+        pair_b_copies[k].wait_recv()
+        sums_b[core, i] += pair_b[i]
+    for sem, group in zip(bx_sems, (far, near)):
+        for k, i in enumerate(others_x):
+            for o in group:
+                dst = wrap(y + o, ny)
+                send("b x", sums_b.at[core, i, dst], slot_bx.at[k, dst], at_x(i), sem)
     hidden_sums(core, 0)
-    hidden_sums(core, 1)
 
     def sums_ready(dst, dist):
         pair_sums[dist].wait_recv()
@@ -429,27 +486,24 @@
             sums_ready,
         )
     next(ring, None)
-    bx_sem, by_sem, ax_sem = send.receive(), send.receive(), send.receive()
-    for k, i in enumerate(others_x):
-        pair_b_copies[k].wait_recv()
-        sums_b[core, i] += pair_b[i]
-        send("b x", sums_b.at[core, i], slot_bx.at[k], at_x(i), bx_sem)
     pair_b_copies[-1].wait_recv()
     sums_b[core, x] += pair_b[x]
+
+    def add_bx(sem, group):
+        if nx > 1 and group:
+            wait_for(slot_bx.at[:, pl.ds(0, len(group))], sem)
+        for o in group:
+            dst = wrap(y + o, ny)
+            total = sums_b[core, x, dst]
+            for k in range(nx - 1):
+                total = total + slot_bx[k, dst]
+            sums_b[core, x, dst] = total
+            if o:
+                send("b y", sums_b.at[core, x, dst], slot_by.at[wrap(o, ny) - 1], at_y(dst), by_sem)
+
     next(ring, None)
-    if nx > 1:
-        wait_for(slot_bx, bx_sem)
-
-    def add_bx(r, _):
-        total = sums_b[core, x, r]
-        for k in range(nx - 1):
-            total = total + slot_bx[k, r]
-        sums_b[core, x, r] = total
-        return 0
-
-    lax.fori_loop(0, ny, add_bx, 0)
-    for k, i in enumerate(others_y):
-        send("b y", sums_b.at[core, x, i], slot_by.at[k], at_y(i), by_sem)
+    add_bx(bx_sems[0], far)
+    add_bx(bx_sems[1], near)
     for _ in ring:
         pass
     for k, i in enumerate(others_x):
@@ -465,7 +519,9 @@
         total = total + slot_by[k]
     hidden_b[core, x, y] = gelu(total + bias)
 
-    hb_y_sem, ha_x_sem, pair_ha_sem, pair_hb_sem = (send.receive() for _ in range(4))
+    ha_x_sem, pair_ha_sem, pair_hb_sem = (send.receive() for _ in range(3))
+    hb_y_sem = send.receive()
+    hb_x_sems = [send.receive() for _ in others_x]
     own = hidden_b.at[core, x, y]
     for i in others_y:
         send("hb y", own, own, at_y(i), hb_y_sem)
@@ -506,12 +562,13 @@
     if ny > 1:
         wait_for(hidden_b.at[0, 0, pl.ds(0, ny - 1)], hb_y_sem)
     own = hidden_b.at[core, x]
-    hb_x = [send("hb x", own, own, at_x(i)) for i in others_x]
+    for i, sem in zip(others_x, hb_x_sems):
+        send("hb x", own, own, at_x(i), sem)
     send("pair hb", own, own, partner, pair_hb_sem)
     next(ring, None)
-    for k, copy in enumerate(hb_x):
-        copy.wait_recv()
+    for k, sem in enumerate(hb_x_sems):
         block = hidden_b.at[core, wrap(x - 1 - k, nx)]
+        wait_for(block, sem)
         send("pair hb", block, block, partner, pair_hb_sem)
     for _ in ring:
         pass
@@ -561,11 +618,11 @@
         def slot(ref):
             return lambda d, t, h: ref.at[c, z_slots[(d, t, h)]]
 
-        yield from reduce_ring(nz, z, at_z, view(mixed), slot(mixed_slot), send, "mixed", mixed_ready, PIECES)
-        kept[z, at, :] = gathered[z, pl.ds(GAINS + c * chunk_rows, chunk_rows), :] + mixed[z, at, :]
-        yield from gather_ring(nz, z, at_z, view(kept), send, "kept", pieces=PIECES)
+        yield from reduce_ring(nz, z, at_z, view(mixed), slot(mixed_slot), send, "mixed", mixed_ready, PIECES, reduce_sems[c])
+        kept[z, at, :] = gathered[z, pl.ds(c * (chunk_rows + GAINS), chunk_rows), :] + mixed[z, at, :]
+        yield from gather_ring(nz, z, at_z, view(kept), send, "kept", pieces=PIECES, recv=gather_sems[c])
         yield "weights"
-        normalize(c, kept, 0, 1)
+        normalize(c, kept, 0, chunk_rows + 1)
 
         def hidden_block(j, _):
             columns = pl.ds(pl.multiple_of(j * width, width), width)
@@ -579,7 +636,7 @@
             wanted_rows = pl.ds(pl.multiple_of(dst * LANES, LANES), LANES)
             final[dst, at, :] = dot3(act_h[at, :], act_l[at, :], ch_out_h[wanted_rows, :], ch_out_l[wanted_rows, :], NT)
 
-        yield from reduce_ring(nz, z, at_z, view(final), slot(final_slot), send, "final", final_ready, PIECES)
+        yield from reduce_ring(nz, z, at_z, view(final), slot(final_slot), send, "final", final_ready, PIECES, reduce_sems[c])
         out[at, :] = kept[z, at, :] + final[z, at, :]
 
     def weights():
@@ -691,7 +748,7 @@
         vmem(CHUNKS, z_slots, piece_rows, LANES),
         vmem(1, hidden_tok),
         vmem(1, hidden_width),
-        pltpu.SemaphoreType.DMA((9,)),
+        pltpu.SemaphoreType.DMA((11,)),
         pltpu.SemaphoreType.DMA((SENDS,)),
         pltpu.SemaphoreType.DMA((RECEIVES,)),
     ]

time: 110 us -> 108 us (0.982); the launches traced: 110 us -> 106 us
  Pallas kernels: 109 us -> 106 us
    pallas_call x1, Pallas kernels: 109 us -> 106 us  [block(): pl.pallas_call(functools.partial(kernel, nz, ny, nx), out_shape=jax.Shape...]
where the time goes in v3:
time: 108 us; the launch traced here: 106 us
  Pallas kernels  106 us (98%)
    pallas_call x1, Pallas kernels, block(): pl.pallas_call(functools.partial(kernel, nz, ny, nx), out_shape=jax.Shape...  106 us

profile of v3, /device:TPU:6, one launch (start us, length us, event | category | flops | bytes accessed | tf_op | source)
XLA Modules:
  0.0 106.4 jit_solution(2547325317179325501)
XLA Ops:
  0.0 105.7 %shard_map.91 = f32[256,128]{1,0:T(8,128)S(1)} custom-call(f32[256,128]{1,0:T(8,128)} %fields.1, f32[1,128]{1,0:T(1,128)} %bitcast.4, f32[1,128]{1,0:T(1,128)} %bitcast.5, f32[384,256]{1,0:T(8,128)} %tok_in.1, f32[384]{0:T(512)} %tok_bias.1, f32[256,384]{1,0:T(8,128)} %tok_out.1, f32[16,768]{1,0:T(8,128)} %ch_in.1, f32[768]{0:T(1024)} %ch_bias.1, ...), custom_call_target="tpu_custom_call" | custom-call | tf_op jit(solution)/shard_map/pallas_call | solution.py:756
  105.7 0.7 copy.11

commit v4 on v3

--- a/solution.py
+++ b/solution.py
@@ -109,7 +109,7 @@
 
 
 def reduce_ring(
-    n, me, device, part, slot, send, group, ready=lambda dst, dist: None, pieces=2, recv=lambda key: None
+    n, me, device, part, slot, send, group, ready=lambda blocks: None, pieces=2, recv=lambda key: None
 ):
     half = n // 2
     flight = {}
@@ -120,9 +120,7 @@
 
     for t in range(1, half + 1):
         dist = half + 1 - t
-        ready(wrap(me + dist, n), dist)
-        if dist != half:
-            ready(wrap(me - dist, n), -dist)
+        ready([wrap(me + k, n) for k in ((dist,) if dist == half else (dist, -dist))])
         for h in range(pieces):
             for d in (1, -1):
                 first = 1 if (d == 1) == (h < pieces // 2) else 2
@@ -135,7 +133,7 @@
                     group, part(dst, h), slot(d, t, h), device(wrap(me + d, n)), recv((d, t, h))
                 )
         yield
-    ready(me, 0)
+    ready([me])
     for key in sorted(flight, key=lambda k: (k[1], k[2])):
         add(me, *key)
 
@@ -386,19 +384,20 @@
         for ring in ring_fields:
             next(ring)
         next(ring_out_y, None)
+        if s == min(3, nz // 2):
+            if nx > 1:
+                wait_for(ch_in_f.at[0, 0, pl.ds(0, nx - 1)], in_x_sem)
+            for h in (0, 1):
+                in_to_partner(y, h)
+            next(ring_in_y, None)
     for c, ring in enumerate(ring_fields):
         for _ in ring:
             pass
         if c == CHUNKS - 1:
             for _ in ring_out_y:
                 pass
-            if nx > 1:
-                wait_for(ch_in_f.at[0, 0, pl.ds(0, nx - 1)], in_x_sem)
             for h in (0, 1):
-                in_to_partner(y, h)
                 out_to_partner(x, h)
-            next(ring_in_y, None)
-            next(ring_out_x, None)
         normalize(c, gathered, c * GAINS, chunk_rows)
 
     def hidden_sums(which, i):
@@ -425,26 +424,15 @@
             offsets = [dist, -dist] + offsets
         offsets = ([half_y] if half_y else []) + offsets
     far, near = ([4, 3, -3, 2], [-2, 1, -1, 0]) if ny == 8 else (list(range(1, ny)), [0])
-    hidden_sums(other, 1)
-    pair_b_copies = []
-    for i in others_x + [x]:
-        pair_b_copies.append(send("pair b", sums_b.at[other, i], pair_b.at[i], partner))
     hidden_sums(other, 0)
     pair_sums = {}
     for k in offsets:
         dst = wrap(y + k, ny)
         pair_sums[k] = send("pair a", sums_a.at[other, dst], pair_a.at[dst], partner)
-    hidden_sums(core, 1)
-    bx_sems = [send.receive(), send.receive()]
-    by_sem, ax_sem = send.receive(), send.receive()
-    for k, i in enumerate(others_x):
-        pair_b_copies[k].wait_recv()
-        sums_b[core, i] += pair_b[i]
-    for sem, group in zip(bx_sems, (far, near)):
-        for k, i in enumerate(others_x):
-            for o in group:
-                dst = wrap(y + o, ny)
-                send("b x", sums_b.at[core, i, dst], slot_bx.at[k, dst], at_x(i), sem)
+    hidden_sums(other, 1)
+    pair_b_copies = []
+    for i in others_x + [x]:
+        pair_b_copies.append(send("pair b", sums_b.at[other, i], pair_b.at[i], partner))
     hidden_sums(core, 0)
 
     def sums_ready(dst, dist):
@@ -483,9 +471,22 @@
             lambda d, t, h: slot_a.at[y_slots[(d, t, h)] // 2, pl.ds((y_slots[(d, t, h)] % 2) * half_x, half_x)],
             send,
             "sums y",
-            sums_ready,
         )
+    if ny != 8:
+        for k in offsets:
+            sums_ready(wrap(y + k, ny), k)
     next(ring, None)
+    hidden_sums(core, 1)
+    bx_sems = [send.receive(), send.receive()]
+    by_sem, ax_sem = send.receive(), send.receive()
+    for k, i in enumerate(others_x):
+        pair_b_copies[k].wait_recv()
+        sums_b[core, i] += pair_b[i]
+    for sem, group in zip(bx_sems, (far, near)):
+        for k, i in enumerate(others_x):
+            for o in group:
+                dst = wrap(y + o, ny)
+                send("b x", sums_b.at[core, i, dst], slot_bx.at[k, dst], at_x(i), sem)
     pair_b_copies[-1].wait_recv()
     sums_b[core, x] += pair_b[x]
 
@@ -608,9 +609,12 @@
     def stages(c):
         at = pl.ds(c * chunk_rows, chunk_rows)
 
-        def mixed_ready(dst, dist):
+        def mixed_ready(blocks):
             if c == 0:
-                mixed[dst] = dot3(tok_out_h[...], tok_out_l[...], hidden_h[dst], hidden_l[dst], NN)
+                right = [jnp.concatenate([ref[dst] for dst in blocks], axis=1) for ref in (hidden_h, hidden_l)]
+                result = dot3(tok_out_h[...], tok_out_l[...], *right, NN)
+                for k, dst in enumerate(blocks):
+                    mixed[dst] = result[:, k * LANES : (k + 1) * LANES]
 
         def view(ref):
             return lambda i, h: ref.at[i, pl.ds(c * chunk_rows + h * piece_rows, piece_rows)]
@@ -632,26 +636,30 @@
 
         lax.fori_loop(0, hidden_width // width, hidden_block, 0)
 
-        def final_ready(dst, dist):
-            wanted_rows = pl.ds(pl.multiple_of(dst * LANES, LANES), LANES)
-            final[dst, at, :] = dot3(act_h[at, :], act_l[at, :], ch_out_h[wanted_rows, :], ch_out_l[wanted_rows, :], NT)
+        def final_ready(blocks):
+            wanted = [pl.ds(pl.multiple_of(dst * LANES, LANES), LANES) for dst in blocks]
+            right = [jnp.concatenate([ref[rows, :] for rows in wanted], axis=0) for ref in (ch_out_h, ch_out_l)]
+            result = dot3(act_h[at, :], act_l[at, :], *right, NT)
+            for k, dst in enumerate(blocks):
+                final[dst, at, :] = result[:, k * LANES : (k + 1) * LANES]
 
         yield from reduce_ring(nz, z, at_z, view(final), slot(final_slot), send, "final", final_ready, PIECES, reduce_sems[c])
         out[at, :] = kept[z, at, :] + final[z, at, :]
 
     def weights():
+        next(ring_out_x, None)
+        yield next(ring_in_y, None)
+        yield
         yield next(ring_in_y, None)
         yield next(ring_out_x, None)
         yield next(ring_in_y, None)
         for _ in ring_out_x:
             pass
         yield
-        yield next(ring_in_y, None)
+        for _ in ring_in_y:
+            pass
         wait_for(ch_out_f.at[0], pair_out_sem)
         lax.fori_loop(0, ny, split_out, 0)
-        yield
-        for _ in ring_in_y:
-            pass
         yield
         wait_for(ch_in_f.at[0], pair_in_sem)
         lax.fori_loop(0, ny, split_in, 0)

time: 108 us -> 106 us (0.981)
  Pallas kernels: 106 us -> 104 us
    pallas_call x1, Pallas kernels: 106 us -> 104 us  [block(): pl.pallas_call(functools.partial(kernel, nz, ny, nx), out_shape=jax.Shape...]
where the time goes in v4:
time: 106 us; the launch traced here: 104 us
  Pallas kernels  104 us (98%)
    pallas_call x1, Pallas kernels, block(): pl.pallas_call(functools.partial(kernel, nz, ny, nx), out_shape=jax.Shape...  104 us

profile of v4, /device:TPU:6, one launch (start us, length us, event | category | flops | bytes accessed | tf_op | source)
XLA Modules:
  0.0 104.4 jit_solution(15303252311515342587)
XLA Ops:
  0.0 103.7 %shard_map.91 = f32[256,128]{1,0:T(8,128)S(1)} custom-call(f32[256,128]{1,0:T(8,128)} %fields.1, f32[1,128]{1,0:T(1,128)} %bitcast.4, f32[1,128]{1,0:T(1,128)} %bitcast.5, f32[384,256]{1,0:T(8,128)} %tok_in.1, f32[384]{0:T(512)} %tok_bias.1, f32[256,384]{1,0:T(8,128)} %tok_out.1, f32[16,768]{1,0:T(8,128)} %ch_in.1, f32[768]{0:T(1024)} %ch_bias.1, ...), custom_call_target="tpu_custom_call" | custom-call | tf_op jit(solution)/shard_map/pallas_call | solution.py:764
  103.7 0.7 copy.11

commit v5 on v4

--- a/solution.py
+++ b/solution.py
@@ -11,6 +11,7 @@
 CORES = 2
 CHUNKS = 2
 PIECES = 4
+SUM_PIECES = 2
 MESH = pl.DeviceIdType.MESH
 F32, BF16 = jnp.float32, jnp.bfloat16
 EPSILON = 1e-05
@@ -36,7 +37,7 @@
 
 NN = ((1,), (0,))
 NT = ((1,), (1,))
-SENDS, RECEIVES = 22, 188
+SENDS, RECEIVES = 22, 160
 
 
 class Sender:
@@ -393,11 +394,6 @@
     for c, ring in enumerate(ring_fields):
         for _ in ring:
             pass
-        if c == CHUNKS - 1:
-            for _ in ring_out_y:
-                pass
-            for h in (0, 1):
-                out_to_partner(x, h)
         normalize(c, gathered, c * GAINS, chunk_rows)
 
     def hidden_sums(which, i):
@@ -502,6 +498,10 @@
             if o:
                 send("b y", sums_b.at[core, x, dst], slot_by.at[wrap(o, ny) - 1], at_y(dst), by_sem)
 
+    for _ in ring_out_y:
+        pass
+    for h in (0, 1):
+        out_to_partner(x, h)
     next(ring, None)
     add_bx(bx_sems[0], far)
     add_bx(bx_sems[1], near)
@@ -587,7 +587,7 @@
 
         lax.fori_loop(0, nx, split_hidden, 0)
 
-    z_slots = slots_of(nz, PIECES)
+    z_slots = slots_of(nz, SUM_PIECES)
     width = 256
 
     def split_out(i, _):
@@ -616,15 +616,16 @@
                 for k, dst in enumerate(blocks):
                     mixed[dst] = result[:, k * LANES : (k + 1) * LANES]
 
-        def view(ref):
-            return lambda i, h: ref.at[i, pl.ds(c * chunk_rows + h * piece_rows, piece_rows)]
+        def view(ref, pieces):
+            size = chunk_rows // pieces
+            return lambda i, h: ref.at[i, pl.ds(c * chunk_rows + h * size, size)]
 
         def slot(ref):
             return lambda d, t, h: ref.at[c, z_slots[(d, t, h)]]
 
-        yield from reduce_ring(nz, z, at_z, view(mixed), slot(mixed_slot), send, "mixed", mixed_ready, PIECES, reduce_sems[c])
+        yield from reduce_ring(nz, z, at_z, view(mixed, SUM_PIECES), slot(mixed_slot), send, "mixed", mixed_ready, SUM_PIECES, reduce_sems[c])
         kept[z, at, :] = gathered[z, pl.ds(c * (chunk_rows + GAINS), chunk_rows), :] + mixed[z, at, :]
-        yield from gather_ring(nz, z, at_z, view(kept), send, "kept", pieces=PIECES, recv=gather_sems[c])
+        yield from gather_ring(nz, z, at_z, view(kept, PIECES), send, "kept", pieces=PIECES, recv=gather_sems[c])
         yield "weights"
         normalize(c, kept, 0, chunk_rows + 1)
 
@@ -643,7 +644,7 @@
             for k, dst in enumerate(blocks):
                 final[dst, at, :] = result[:, k * LANES : (k + 1) * LANES]
 
-        yield from reduce_ring(nz, z, at_z, view(final), slot(final_slot), send, "final", final_ready, PIECES, reduce_sems[c])
+        yield from reduce_ring(nz, z, at_z, view(final, SUM_PIECES), slot(final_slot), send, "final", final_ready, SUM_PIECES, reduce_sems[c])
         out[at, :] = kept[z, at, :] + final[z, at, :]
 
     def weights():
@@ -713,8 +714,8 @@
     channels = nz * LANES
     y_rows = hidden_tok // (CORES * ny)
     x_width = channels // (2 * nx)
-    z_slots = max(1, len(slots_of(nz, PIECES)))
-    piece_rows = rows // (PIECES * CHUNKS)
+    z_slots = max(1, len(slots_of(nz, SUM_PIECES)))
+    piece_rows = rows // (SUM_PIECES * CHUNKS)
 
     def vmem(*shape, kind=F32):
         return pltpu.VMEM(shape, kind)

time: 106 us -> 105 us (level)
  no operation moved by 1% of the time
where the time goes in v5:
time: 105 us; the launch traced here: 104 us
  Pallas kernels  103 us (98%)
    pallas_call x1, Pallas kernels, block(): pl.pallas_call(functools.partial(kernel, nz, ny, nx), out_shape=jax.Shape...  103 us

profile of v5, /device:TPU:6, one launch (start us, length us, event | category | flops | bytes accessed | tf_op | source)
XLA Modules:
  0.0 103.7 jit_solution(11766052007085138570)
XLA Ops:
  0.0 103.0 %shard_map.91 = f32[256,128]{1,0:T(8,128)S(1)} custom-call(f32[256,128]{1,0:T(8,128)} %fields.1, f32[1,128]{1,0:T(1,128)} %bitcast.4, f32[1,128]{1,0:T(1,128)} %bitcast.5, f32[384,256]{1,0:T(8,128)} %tok_in.1, f32[384]{0:T(512)} %tok_bias.1, f32[256,384]{1,0:T(8,128)} %tok_out.1, f32[16,768]{1,0:T(8,128)} %ch_in.1, f32[768]{0:T(1024)} %ch_bias.1, ...), custom_call_target="tpu_custom_call" | custom-call | tf_op jit(solution)/shard_map/pallas_call | solution.py:765
  103.0 0.7 copy.11
